TPU v7x, 128 devices: a whole 4x4x4 slice. The times are simulated.
128 devices in a mesh: dp: 128 (over z, y, x, core).
Axes of the slice: x: 4, y: 4, z: 4, core: 2. Of those that a mesh axis runs over, the one named last changes fastest.
Arguments:
- query_feat: bfloat16 [32768, 512], P('dp')
- item_feat: bfloat16 [32768, 512], P('dp')
- log_q: float32 [32768], P('dp')
- w_query_in: bfloat16 [512, 256], replicated
- w_query_out: bfloat16 [256, 128], replicated
- w_item_in: bfloat16 [512, 256], replicated
- w_item_out: bfloat16 [256, 128], replicated
Outputs:
- output 1: float32 [1], replicated
- output 2: float32 [512, 256], replicated
- output 3: float32 [256, 128], replicated
- output 4: float32 [512, 256], replicated
- output 5: float32 [256, 128], replicated
All inputs are finite; a program needn't handle non-finite values.
Results may differ from a plain program's by a relative error of at most 0.00699549.
Values are sent between devices in bfloat16 or wider.
A program may use at most 1 GiB of HBM per device.

v0:
```python
import jax
import jax.numpy as jnp
from jax import lax
from jax.sharding import PartitionSpec as P

value_a11 = 0.05
NORM_EPS = 1e-6


def tower_forward(feat_rows, w_in, w_out):
    pre_act = jnp.dot(feat_rows, w_in, preferred_element_type=jnp.float32)
    hidden = jnp.maximum(pre_act, 0.0).astype(jnp.bfloat16)
    embed = jnp.dot(hidden, w_out, preferred_element_type=jnp.float32)
    inv_norm = lax.rsqrt(jnp.sum(embed * embed, axis=-1, keepdims=True) + NORM_EPS)
    return pre_act, hidden, inv_norm, embed * inv_norm


def tower_backward(feat_rows, w_out, pre_act, hidden, inv_norm, unit_vec, d_unit):
    d_embed = inv_norm * (d_unit - unit_vec * jnp.sum(unit_vec * d_unit, axis=-1, keepdims=True))
    d_embed_bf = d_embed.astype(jnp.bfloat16)
    grad_out = jnp.einsum('bh,be->he', hidden, d_embed_bf, preferred_element_type=jnp.float32)
    d_hidden = jnp.einsum('be,he->bh', d_embed_bf, w_out, preferred_element_type=jnp.float32)
    d_pre = jnp.where(pre_act > 0, d_hidden, 0.0).astype(jnp.bfloat16)
    grad_in = jnp.einsum('bf,bh->fh', feat_rows, d_pre, preferred_element_type=jnp.float32)
    return grad_in, grad_out


def softmax_grads(query_bf, items_all, logq_all, row_offset):
    local_rows, embed_dim = query_bf.shape
    total_rows = items_all.shape[0]
    block_rows = min(local_rows, 256)
    num_blocks = local_rows // block_rows
    grad_scale = 1.0 / (value_a11 * total_rows)
    col_ids = lax.broadcasted_iota(jnp.int32, (1, total_rows), 1)
    row_iota = lax.broadcasted_iota(jnp.int32, (block_rows, 1), 0)
    query_blocks = query_bf.reshape(num_blocks, block_rows, embed_dim)

    def block_step(d_item_acc, inputs):
        block_index, query_blk = inputs
        logits = jnp.einsum('qe,ke->qk', query_blk, items_all, preferred_element_type=jnp.float32) / value_a11 - logq_all[None, :]
        is_pos = (row_offset + block_index * block_rows + row_iota) == col_ids
        row_max = jnp.max(logits, axis=1, keepdims=True)
        log_norm = row_max + jnp.log(jnp.sum(jnp.exp(logits - row_max), axis=1, keepdims=True))
        pos_logit = jnp.sum(jnp.where(is_pos, logits, 0.0), axis=1, keepdims=True)
        prob_rows = jnp.exp(logits - log_norm)
        grad_logits = jnp.where(is_pos, prob_rows - 1.0, prob_rows).astype(jnp.bfloat16)
        d_query_blk = jnp.einsum('qk,ke->qe', grad_logits, items_all, preferred_element_type=jnp.float32) * grad_scale
        d_item_acc = d_item_acc + jnp.einsum('qk,qe->ke', grad_logits, query_blk, preferred_element_type=jnp.float32)
        return d_item_acc, (jnp.sum(log_norm - pos_logit), d_query_blk)

    acc_init = jnp.zeros((total_rows, embed_dim), jnp.float32)
    d_item_acc, (loss_parts, d_query_blocks) = lax.scan(block_step, acc_init, (jnp.arange(num_blocks), query_blocks))
    return jnp.sum(loss_parts), d_query_blocks.reshape(local_rows, embed_dim), d_item_acc * grad_scale


def solution(mesh):
    group = mesh.shape['dp']

    def local_step(query_feat, item_feat, log_q, w_query_in, w_query_out, w_item_in, w_item_out):
        local_rows = query_feat.shape[0]
        total_rows = local_rows * group
        q_pre, q_hidden, q_inv, q_unit = tower_forward(query_feat, w_query_in, w_query_out)
        v_pre, v_hidden, v_inv, v_unit = tower_forward(item_feat, w_item_in, w_item_out)
        items_all = lax.all_gather(v_unit.astype(jnp.bfloat16), 'dp', axis=0, tiled=True)
        logq_all = lax.all_gather(log_q, 'dp', axis=0, tiled=True)
        row_offset = lax.axis_index('dp') * local_rows
        loss_sum, d_query, d_item_part = softmax_grads(q_unit.astype(jnp.bfloat16), items_all, logq_all, row_offset)
        d_item = lax.psum_scatter(d_item_part, 'dp', scatter_dimension=0, tiled=True)
        grad_query_in, grad_query_out = tower_backward(query_feat, w_query_out, q_pre, q_hidden, q_inv, q_unit, d_query)
        grad_item_in, grad_item_out = tower_backward(item_feat, w_item_out, v_pre, v_hidden, v_inv, v_unit, d_item)
        loss = jnp.reshape(lax.psum(loss_sum, 'dp') / total_rows, (1,))
        return (loss, lax.psum(grad_query_in, 'dp'), lax.psum(grad_query_out, 'dp'), lax.psum(grad_item_in, 'dp'), lax.psum(grad_item_out, 'dp'))

    return jax.shard_map(local_step, mesh=mesh, in_specs=(P('dp', None), P('dp', None), P('dp'), P(), P(), P(), P()), out_specs=(P(), P(), P(), P(), P()), check_vma=False)
```

profile of v0, /device:TPU:1, one launch (start us, length us, event | category | flops | bytes accessed | tf_op | source)
XLA Modules:
  0.0 990.9 jit_solution(787777601133963622)
XLA Ops:
  7.2 0.0 copy-start
  7.2 0.0 all-gather.3.cloned.1.call-start
  7.2 1.3 fusion.20
  8.5 1.1 multiply_reduce_fusion.2
  9.6 0.6 multiply_convert_fusion.2
  10.3 0.0 all-gather.3.cloned.1.call-update
  10.3 0.0 reduce-scatter.2.cloned.1.call-start
  10.3 38.9 %all-gather = f32[128,1,256]{2,1,0:T(1,128)S(1)} all-gather(f32[1,1,256]{2,1,0:T(1,128)} %bitcast.26), channel_id=1, replica_groups=mesh['dp'=128] {'dp'}, dimensions={0}, use_global_device_ids=true | all-gather | bytes 132096 | tf_op jit(solution)/shard_map/all_gather | solution.py:65
  49.2 0.0 copy-done
  49.2 1.2 fusion.19
  50.4 1.1 multiply_reduce_fusion.3
  51.5 40.0 %all-gather.3.cloned.1.call-done = bf16[32768,128]{0,1:T(8,128)(2,1)} async-done(((bf16[256,128]{0,1:T(8,128)(2,1)}), bf16[32768,128]{0,1:T(8,128)(2,1)}) %all-gather.3.cloned.1.call-update) | async-done | bytes 8388624 | tf_op jit(solution)/shard_map/all_gather | solution.py:64
  91.5 16.6 %fusion.18 = (f32[256]{0:T(256)S(1)}, f32[256,32768]{1,0:T(8,128)}) fusion(f32[32768]{0:T(1024)S(1)} %bitcast.25, bf16[32768,128]{0,1:T(8,128)(2,1)} %all-gather.3.cloned.1.call-done, f32[256,128]{0,1:T(8,128)S(1)} %get-tuple-element.56, f32[256]{0:T(256)S(1)} %add_rsqrt_fusion.1), kind=kOutput, calls=%fused_computation.44 | convolution fusion | flops 2172714752 | bytes 42207232 | tf_op jit(solution)/shard_map/while/body/eval_jaxpr/qe,ke->qk/dot_general | solution.py:40
  108.1 0.0 copy-start.1
  108.1 17.3 %select_reduce_fusion = (f32[256]{0:T(256)S(1)}, f32[256]{0:T(256)S(1)}) fusion(f32[256,32768]{1,0:T(8,128)} %get-tuple-element.58, s32[256]{0:T(256)S(1)} %iota_add_fusion, f32[256]{0:T(256)S(1)} %get-tuple-element.57), kind=kLoop, calls=%fused_computation.5 | loop fusion | flops 41942528 | bytes 33558528 | tf_op jit(solution)/shard_map/while/body/eval_jaxpr/reduce_sum | solution.py:44
  125.4 0.6 subtract_reduce_fusion
  126.0 2.4 copy-done.1
  128.3 10.3 %fusion.1 = bf16[256,32768]{1,0:T(8,128)(2,1)} fusion(f32[256,32768]{1,0:T(8,128)S(1)} %copy-done.1, f32[256]{0:T(256)S(1)} %get-tuple-element.52, s32[256]{0:T(256)S(1)} %iota_add_fusion), kind=kLoop, calls=%fused_computation.4 | loop fusion | flops 41943040 | bytes 50333696 | tf_op jit(solution)/shard_map/while/body/eval_jaxpr/convert_element_type | solution.py:46
  138.7 14.0 %convolution_multiply_fusion.1 = f32[32768,128]{0,1:T(8,128)} fusion(bf16[256,32768]{1,0:T(8,128)(2,1)} %fusion.1, f32[256,128]{0,1:T(8,128)S(1)} %get-tuple-element.56, f32[256]{0:T(256)S(1)} %add_rsqrt_fusion.1), kind=kOutput, calls=%fused_computation.3 | convolution fusion | flops 2151743488 | bytes 33686528 | tf_op jit(solution)/shard_map/while/body/eval_jaxpr/qk,qe->ke/dot_general | solution.py:48
  152.7 0.0 copy-start.3
  152.7 0.0 copy-start.2
  152.7 0.0 copy-start.4
  152.7 0.0 reduce-scatter.2.cloned.1.call-update
  152.7 0.2 all-reduce.3.cloned.1.call-start
  153.0 13.9 %multiply_reduce_fusion.1 = (f32[256]{0:T(256)S(1)}, f32[256,128]{0,1:T(8,128)S(1)}) fusion(f32[256,128]{0,1:T(8,128)S(1)} %get-tuple-element.56, f32[256]{0:T(256)S(1)} %add_rsqrt_fusion.1, bf16[256,32768]{1,0:T(8,128)(2,1)} %fusion.1, bf16[32768,128]{0,1:T(8,128)(2,1)} %all-gather.3.cloned.1.call-done), kind=kOutput, calls=%fused_computation.22 | convolution fusion | flops 2147614464 | bytes 25430016 | tf_op jit(solution)/shard_map/while/body/eval_jaxpr/qk,ke->qe/dot_general | solution.py:47
  166.9 0.9 fusion.8
  167.8 0.0 copy-done.3
  167.8 1.2 convolution_bitcast_fusion.1
  169.0 649.6 %reduce-scatter.2.cloned.1.call-done = f32[256,128]{0,1:T(8,128)} async-done(((f32[32768,128]{0,1:T(8,128)}), f32[256,128]{0,1:T(8,128)}) %reduce-scatter.2.cloned.1.call-update) | async-done | bytes 131088 | tf_op jit(solution)/shard_map/reduce_scatter | solution.py:68
  818.6 0.9 multiply_reduce_fusion
  819.5 0.9 multiply_convert_fusion
  820.5 0.9 fusion.10
  821.3 0.0 copy-done.2
  821.3 0.0 copy-done.4
  821.4 1.2 convolution_bitcast_fusion
  822.6 0.0 all-reduce.3.cloned.1.call-update
  822.6 69.7 %psum.35 = f32[]{:T(128)} all-reduce(f32[]{:T(128)} %get-tuple-element.51), channel_id=1, replica_groups=mesh['dp'=128] {'dp'}, use_global_device_ids=true, to_apply=%region_6.7 | all-reduce | flops 1 | bytes 8 | tf_op jit(solution)/shard_map/psum | solution.py:71
  892.9 83.1 %all-reduce.3.cloned.1.call-done = (f32[512,256]{0,1:T(8,128)}, f32[256,128]{1,0:T(8,128)}, f32[512,256]{0,1:T(8,128)}, f32[256,128]{1,0:T(8,128)}) async-done(((f32[512,256]{0,1:T(8,128)}, f32[256,128]{1,0:T(8,128)}, f32[512,256]{0,1:T(8,128)}, f32[256,128]{1,0:T(8,128)}), (f32[512,256]{0,1:T(8,128)}, f32[256,128]{1,0:T(8,128)}, f32[512,256]{0,1:T(8,128)}, ...) | async-done | bytes 1310736 | tf_op jit(solution)/shard_map/psum | solution.py:72
  976.0 2.0 copy.16
  978.1 2.0 copy.17
  980.1 1.6 copy.23
  981.7 1.6 copy.24
  (4 shorter events, 0.0 us)
Async XLA Ops:
  7.2 42.0 %copy-start = (bf16[256,512]{1,0:T(8,128)(2,1)S(1)}, bf16[256,512]{1,0:T(8,128)(2,1)}, u32[]{:S(2)}) copy-start(bf16[256,512]{1,0:T(8,128)(2,1)} %param.7) | copy-start | bytes 786436
  7.2 84.3 %all-gather.3.cloned.1.call-start = ((), (), s32[]{:S(2)}) async-start(), calls=%async_computation.1 | async-start | bytes 8454144 | tf_op jit(solution)/shard_map/all_gather | solution.py:64
  10.3 808.3 %reduce-scatter.2.cloned.1.call-start = ((), (), s32[]{:S(2)}) async-start(), calls=%async_computation.2 | async-start | bytes 16908288 | tf_op jit(solution)/shard_map/reduce_scatter | solution.py:68
  108.1 20.2 %copy-start.1 = (f32[256,32768]{1,0:T(8,128)S(1)}, f32[256,32768]{1,0:T(8,128)}, u32[]{:S(2)}) copy-start(f32[256,32768]{1,0:T(8,128)} %get-tuple-element.58) | copy-start | bytes 100663296
  152.7 15.1 %copy-start.3 = (bf16[256,128]{1,0:T(8,128)(2,1)S(1)}, bf16[256,128]{1,0:T(8,128)(2,1)}, u32[]{:S(2)}) copy-start(bf16[256,128]{1,0:T(8,128)(2,1)} %param.11) | copy-start | bytes 196612
  152.7 668.7 %copy-start.2 = (bf16[256,512]{1,0:T(8,128)(2,1)S(1)}, bf16[256,512]{1,0:T(8,128)(2,1)}, u32[]{:S(2)}) copy-start(bf16[256,512]{1,0:T(8,128)(2,1)} %param.8) | copy-start | bytes 786436
  152.7 668.7 %copy-start.4 = (bf16[256,128]{1,0:T(8,128)(2,1)S(1)}, bf16[256,128]{1,0:T(8,128)(2,1)}, u32[]{:S(2)}) copy-start(bf16[256,128]{1,0:T(8,128)(2,1)} %param.13) | copy-start | bytes 196612
  152.7 823.3 %all-reduce.3.cloned.1.call-start = ((), (), s32[]{:S(2)}) async-start(), calls=%async_computation.3 | async-start | bytes 2621440 | tf_op jit(solution)/shard_map/psum | solution.py:72
Sparse Core Ops, SparseCore 0:
  11.4 80.0 all-gather.2
  152.8 665.6 reduce-scatter.1
  824.5 151.4 all-reduce.2
where the time goes:
time: 992 us; the launch traced here: 991 us
  waiting for transfers between devices  773 us (78%)
  blocking collectives  109 us (11%)
  matrix products  53.3 us (5%)
  other arithmetic  30.8 us (3%)
  between operations  15.6 us (2%)
    reduce_scatter x1, waiting for transfers between devices, local_step(): lax.psum_scatter(d_item_part, 'dp', scatter_dimension=0, tiled=True)  650 us
    psum x1, waiting for transfers between devices, local_step(): lax.psum(grad_query_in, 'dp')  83.1 us
    psum x1, blocking collectives, local_step(): loss = jnp.reshape(lax.psum(loss_sum, 'dp') / total_rows, (1,))  69.7 us
    all_gather x1, waiting for transfers between devices, local_step(): lax.all_gather(v_unit.astype(jnp.bfloat16), 'dp', axis=0, tiled=True)  40 us
    all_gather x1, blocking collectives, local_step(): logq_all = lax.all_gather(log_q, 'dp', axis=0, tiled=True)  38.9 us
  transfers between devices with their start and end apart: 3, of which 3 were waited for; matrix products, arithmetic and copies ran while one was open for 2% of the time, Pallas kernels for 0%

commit v1 on v0

v1 whole, which is shorter than its diff:
```python
import functools

import jax
import jax.numpy as jnp
from jax import lax
from jax.experimental import pallas as pl
from jax.experimental.pallas import tpu as pltpu
from jax.sharding import PartitionSpec as P

TEMP = 0.05
NORM_EPS = 1e-6
LOG2E = 1.4426950408889634
BOUND = 20.25
F32 = jnp.float32
BF16 = jnp.bfloat16
NA, NB, NC = 8, 16, 8
STEP = (0, 1, 3, 2)
BACK = (0, 2, 1, 3)
INV_A = [2 * BACK[s // 2] + s % 2 for s in range(NA)]
INV_B = [4 * BACK[t // 4] + t % 4 for t in range(NB)]


def rel_a(r, s):
    dy = (STEP[r // 2] - STEP[s // 2]) % 4
    return 2 * STEP.index(dy) + (r % 2 + s % 2) % 2


def nt(a, b):
    return lax.dot_general(a, b, (((1,), (1,)), ((), ())), preferred_element_type=F32)


def tn(a, b):
    return lax.dot_general(a, b, (((0,), (0,)), ((), ())), preferred_element_type=F32)


def nn(a, b):
    return jnp.dot(a, b, preferred_element_type=F32)


def forward(x, w_in, w_out, pre_s, hid_s, inv_s, unit_s, out):
    pre = nn(x[...], w_in[...])
    hid = jnp.maximum(pre, 0.0).astype(BF16)
    emb = nn(hid, w_out[...])
    inv = lax.rsqrt(jnp.sum(emb * emb, axis=-1, keepdims=True) + NORM_EPS)
    unit = emb * inv
    out[0] = unit.astype(BF16)
    pre_s[...] = pre
    hid_s[...] = hid
    inv_s[...] = jnp.broadcast_to(inv, unit.shape)
    unit_s[...] = unit


def backward(x, w_out, pre_s, hid_s, inv_s, unit_s, d_unit):
    unit = unit_s[...]
    d_emb = inv_s[...] * (d_unit - unit * jnp.sum(unit * d_unit, axis=-1, keepdims=True))
    d_emb = d_emb.astype(BF16)
    g_out = tn(hid_s[...], d_emb)
    d_hid = nt(d_emb, w_out[...])
    d_pre = jnp.where(pre_s[...] > 0, d_hid, 0.0).astype(BF16)
    g_in = tn(x[...], d_pre)
    return g_in, g_out


def kernel(total_rows, qx, vx, lq, wqi, wqo, wvi, wvo,
           loss_o, gqi_o, gqo_o, gvi_o, gvo_o,
           u_all, v_all, lq_all, kcol, e_all, zacc, zs, rz, dut, dur, dvs, dvr,
           q_pre, q_hid, q_inv, q_unit, v_pre, v_hid, v_inv, v_unit,
           gq, gv, pq, pv, hq, hv, rq, rv, oq, ov, xq, xv, fq, fv,
           us, ur, vs, vr, ls, lr, zss, zsr, dus, durs, dvss, dvsr,
           ps, pr, r1s, r1r, r2s, r2r, r3s, r3r, r4s, r4r):
    me = lax.axis_index("dp")
    core = me % 2
    x = (me // 2) % 4
    y = (me // 8) % 4
    z = me // 32
    lo = ((z + 1) // 2) % 2
    hi = z // 2
    scale = 1.0 / (TEMP * total_rows)

    def a_dev(s):
        zz = z + (s % 2) * (1 - 2 * (z % 2))
        return zz * 32 + ((y + STEP[s // 2]) % 4) * 8 + x * 2 + core

    def b_dev(t):
        i = t // 4
        step = STEP[i] if isinstance(t, int) else i + (i // 2) * (1 - 2 * (i % 2))
        zz = z + ((t // 2) % 2) * (3 - 2 * z)
        return zz * 32 + y * 8 + ((x + step) % 4) * 2 + (core + t % 2) % 2

    def copy(src, dst, ssem, rsem, dev):
        return pltpu.make_async_remote_copy(src_ref=src, dst_ref=dst, send_sem=ssem, recv_sem=rsem,
                                            device_id=(dev,), device_id_type=pl.DeviceIdType.MESH)

    sent = []

    def send(src, dst, ssem, rsem, dev):
        c = copy(src, dst, ssem, rsem, dev)
        c.start()
        sent.append(c)

    def arrived(dst, ssem, rsem):
        copy(dst, dst, ssem, rsem, me).wait_recv()

    barrier = pltpu.get_barrier_semaphore()
    for s in range(1, NA):
        pl.semaphore_signal(barrier, inc=1, device_id=(a_dev(s),), device_id_type=pl.DeviceIdType.MESH)
    for t in range(1, NB):
        pl.semaphore_signal(barrier, inc=1, device_id=(b_dev(t),), device_id_type=pl.DeviceIdType.MESH)

    forward(vx, wvi, wvo, v_pre, v_hid, v_inv, v_unit, v_all)
    pl.semaphore_wait(barrier, NA + NB - 2)
    for t in range(1, NB):
        send(lq, lq_all.at[INV_B[t]], ls.at[t], lr.at[INV_B[t]], b_dev(t))
    forward(qx, wqi, wqo, q_pre, q_hid, q_inv, q_unit, u_all)
    for t in range(1, NB):
        send(v_all.at[0], v_all.at[INV_B[t]], vs.at[t], vr.at[INV_B[t]], b_dev(t))
        if t % 2 == 1:
            s = t // 2
            if s >= 1:
                send(u_all.at[0], u_all.at[INV_A[s]], us.at[s], ur.at[INV_A[s]], a_dev(s))
    lq_all[0] = lq[...]
    zacc[...] = jnp.zeros_like(zacc)

    low = lq[...]
    for t in range(1, NB):
        arrived(lq_all.at[t], ls.at[t], lr.at[t])
        low = jnp.minimum(low, lq_all[t])
    low = jnp.min(low, axis=1, keepdims=True)

    def column(t, c):
        row = LOG2E * ((lq_all[t] - low) + BOUND)
        kcol[t] = jnp.transpose(jnp.broadcast_to(row, (128, 256)))
        return c

    lax.fori_loop(0, NB, column, 0)
    for s in range(1, NA):
        arrived(u_all.at[s], us.at[s], ur.at[s])

    c2 = LOG2E / TEMP

    def logits(t, c):
        @pl.when(t > 0)
        def _():
            arrived(v_all.at[t], vs.at[t], vr.at[t])

        vt = v_all[t]
        kc = kcol[t]
        kc = jnp.concatenate([kc, kc], axis=1)
        for s in range(NA):
            e = jnp.exp2(nt(vt, u_all[s]) * c2 - kc)
            e_all[t, s] = e
            zacc[s] += jnp.sum(e.reshape(32, 8, 256), axis=0)
        return c

    lax.fori_loop(0, NB, logits, 0)

    rows = [jnp.sum(zacc[s], axis=0, keepdims=True) for s in range(NA)]
    zs[0] = jnp.concatenate(rows + [jnp.broadcast_to(low, (8, 256))], axis=0)
    eye = lax.broadcasted_iota(jnp.int32, (256, 256), 0) == lax.broadcasted_iota(jnp.int32, (256, 256), 1)
    dots = jnp.sum(jnp.where(eye, nt(v_all[0], u_all[0]), 0.0), axis=0, keepdims=True)
    for s in range(1, NA):
        send(zs.at[0], zs.at[INV_A[s]], zss.at[s], zsr.at[INV_A[s]], a_dev(s))
    for s in range(1, NA):
        arrived(zs.at[s], zss.at[s], zsr.at[s])

    lows = [zs[s, 8:9, :] for s in range(NA)]
    least = functools.reduce(jnp.minimum, lows)
    fac = [jnp.exp(least - w) for w in lows]
    tot = []
    for r in range(NA):
        acc = None
        for s in range(NA):
            k = rel_a(r, s)
            term = fac[s] * zs[s, k:k + 1, :]
            acc = term if acc is None else acc + term
        tot.append(acc)
    for r in range(NA):
        rz[r:r + 1, :] = fac[0] / tot[r]
    loss_rows = ((BOUND - least) + jnp.log(tot[0])) - (dots / TEMP - lq[...])
    loss_loc = jnp.sum(loss_rows, axis=1, keepdims=True)

    def grads(t, diag):
        vt = v_all[t]
        dv = None
        for s in range(NA):
            p = e_all[t, s] * rz[s:s + 1, :]
            if diag and s == 0:
                p = jnp.where(eye, p - 1.0, p)
            g = p.astype(BF16)
            d = nn(g, u_all[s])
            dv = d if dv is None else dv + d
            du = tn(vt, g)
            if diag:
                dut[s] = du
            else:
                dut[s] += du
        dvs[t] = dv

    def dv_copy(t):
        i = t // 4
        back = i + ((i + 1) // 2) * (3 - 2 * i) * (1 - i // 3)
        slot = 4 * back + t % 4
        return copy(dvs.at[t], dvr.at[slot], dvss.at[t], dvsr.at[slot], b_dev(t))

    grads(0, True)

    def step(t, c):
        grads(t, False)

        @pl.when(t > 1)
        def _():
            dv_copy(t - 1).start()
        return c

    lax.fori_loop(1, NB, step, 0)
    for s in range(1, NA):
        send(dut.at[s], dur.at[INV_A[s]], dus.at[s], durs.at[INV_A[s]], a_dev(s))
    dv_copy(jnp.int32(NB - 1)).start()

    du = dut[0]
    for s in range(1, NA):
        arrived(dur.at[s], dus.at[s], durs.at[s])
        du = du + dur[s]
    d_unit = jnp.transpose(du) * scale
    g_in, g_out = backward(qx, wqo, q_pre, q_hid, q_inv, q_unit, d_unit)

    def pack(buf, g_in, g_out):
        buf[0, 0:512, :] = g_in[:, 0:128]
        buf[0, 512:640, :] = g_in[0:128, 128:256]
        buf[1, 0:384, :] = g_in[128:512, 128:256]
        buf[1, 384:640, :] = g_out

    pack(gq, g_in, g_out)
    lt = jnp.broadcast_to(loss_loc, (8, 128))
    gq[0, 640:648, :] = lt
    gq[1, 640:648, :] = lt
    send(gq.at[(core + 1) % 2], pq, ps.at[0], pr.at[0], b_dev(1))

    def add_dv(t, acc):
        arrived(dvr.at[t], dvss.at[t], dvsr.at[t])
        return acc + dvr[t]

    dv = lax.fori_loop(1, NB, add_dv, dvs[0])
    g_in, g_out = backward(vx, wvo, v_pre, v_hid, v_inv, v_unit, dv * scale)
    pack(gv, g_in, g_out)
    send(gv.at[(core + 1) % 2], pv, ps.at[1], pr.at[1], b_dev(1))

    a_me, b_me = y * 2 + lo, x * 2 + hi

    def a_idx(s):
        return ((y + STEP[s // 2]) % 4) * 2 + (lo + s % 2) % 2

    def c_idx(t):
        return ((x + STEP[t // 2]) % 4) * 2 + (hi + t % 2) % 2

    def c_dev(t):
        return b_dev(2 * t)

    paths = (
        (gq, pq, hq, rq, oq, xq, fq, c_dev, c_idx, b_me, a_dev, 88, 0),
        (gv, pv, hv, rv, ov, xv, fv, a_dev, a_idx, a_me, c_dev, 80, 1),
    )
    for g, p, h, r, o, xx, f, dev1, idx1, mine, dev2, n, w in paths:
        arrived(p, ps.at[w], pr.at[w])
        h[:, 0:80, :] = (g[core, 0:640, :] + p[0:640, :]).reshape(8, 80, 128)
        if n > 80:
            extra = g[core, 640:648, :] + p[640:648, :]
            for k in range(8):
                h[k, 80:88, :] = extra
        for s in range(1, 8):
            k = INV_A[s]
            send(h.at[idx1(s)], r.at[k], r1s.at[w, s], r1r.at[w, k], dev1(s))
    for g, p, h, r, o, xx, f, dev1, idx1, mine, dev2, n, w in paths:
        acc = h[mine]
        for s in range(1, 8):
            arrived(r.at[s], r1s.at[w, s], r1r.at[w, s])
            acc = acc + r[s]
        o[...] = acc
        for s in range(1, 8):
            k = INV_A[s]
            send(o, xx.at[k], r2s.at[w, s], r2r.at[w, k], dev2(s))
    for g, p, h, r, o, xx, f, dev1, idx1, mine, dev2, n, w in paths:
        acc = o[...]
        for s in range(1, 8):
            arrived(xx.at[s], r2s.at[w, s], r2r.at[w, s])
            acc = acc + xx[s]
        f[core, mine] = acc
        for s in range(1, 8):
            k = INV_A[s]
            send(f.at[core, mine], f.at[core, mine], r3s.at[w, s], r3r.at[w, k], dev1(s))
        send(f.at[core, mine], f.at[core, mine], r4s.at[w, 0], r4r.at[w, 0], b_dev(1))
        if n > 80:
            loss_o[0] = acc[80, 0] * (1.0 / total_rows)
    other = (core + 1) % 2
    for g, p, h, r, o, xx, f, dev1, idx1, mine, dev2, n, w in paths:
        for s in range(1, 8):
            k = idx1(s)
            arrived(f.at[core, k], r3s.at[w, s], r3r.at[w, s])
            send(f.at[core, k], f.at[core, k], r4s.at[w, s], r4r.at[w, s], b_dev(1))
    for g, p, h, r, o, xx, f, dev1, idx1, mine, dev2, n, w in paths:
        arrived(f.at[other, mine], r4s.at[w, 0], r4r.at[w, 0])
        for s in range(1, 8):
            arrived(f.at[other, idx1(s)], r4s.at[w, s], r4r.at[w, s])
        go_in, go_out = (gqi_o, gqo_o) if w == 0 else (gvi_o, gvo_o)
        first = f[0, :, 0:80, :].reshape(640, 128)
        second = f[1, :, 0:80, :].reshape(640, 128)
        go_in[:, 0:128] = first[0:512]
        go_in[0:128, 128:256] = first[512:640]
        go_in[128:512, 128:256] = second[0:384]
        go_out[...] = second[384:640]

    for c in sent:
        c.wait_send()

    def drain(t, c):
        dv_copy(t).wait_send()
        return c

    lax.fori_loop(1, NB, drain, 0)


def solution(mesh):
    group = mesh.shape["dp"]

    def local_step(query_feat, item_feat, log_q, w_query_in, w_query_out, w_item_in, w_item_out):
        local_rows = query_feat.shape[0]
        vm = lambda *s: pltpu.VMEM(s, F32)
        vb = lambda *s: pltpu.VMEM(s, BF16)
        sem = lambda *s: pltpu.SemaphoreType.DMA(s)
        scratch = [
            vb(NA, 256, 128), vb(NB, 256, 128), vm(NB, 1, 256), vm(NB, 256, 128), vm(NB, NA, 256, 256),
            vm(NA, 8, 256), vm(NA, 16, 256), vm(NA, 256), vm(NA, 128, 256), vm(NA, 128, 256),
            vm(NB, 256, 128), vm(NB, 256, 128),
            vm(256, 256), vb(256, 256), vm(256, 128), vm(256, 128),
            vm(256, 256), vb(256, 256), vm(256, 128), vm(256, 128),
            vm(2, 648, 128), vm(2, 640, 128), vm(648, 128), vm(640, 128),
            vm(8, 88, 128), vm(8, 80, 128), vm(8, 88, 128), vm(8, 80, 128),
            vm(88, 128), vm(80, 128), vm(8, 88, 128), vm(8, 80, 128),
            vm(2, 8, 88, 128), vm(2, 8, 80, 128),
            sem(NA), sem(NA), sem(NB), sem(NB), sem(NB), sem(NB), sem(NA), sem(NA),
            sem(NA), sem(NA), sem(NB), sem(NB),
            sem(2), sem(2), sem(2, 8), sem(2, 8), sem(2, 8), sem(2, 8), sem(2, 8), sem(2, 8), sem(2, 8), sem(2, 8),
        ]
        vspec = pl.BlockSpec(memory_space=pltpu.VMEM)
        return pl.pallas_call(
            functools.partial(kernel, local_rows * group),
            out_shape=(jax.ShapeDtypeStruct((1,), F32),
                       jax.ShapeDtypeStruct((512, 256), F32), jax.ShapeDtypeStruct((256, 128), F32),
                       jax.ShapeDtypeStruct((512, 256), F32), jax.ShapeDtypeStruct((256, 128), F32)),
            in_specs=[vspec] * 7,
            out_specs=(pl.BlockSpec(memory_space=pltpu.SMEM), vspec, vspec, vspec, vspec),
            scratch_shapes=scratch,
            compiler_params=pltpu.CompilerParams(collective_id=0, has_side_effects=True,
                                                 vmem_limit_bytes=62 * 1024 * 1024),
        )(query_feat, item_feat, log_q.reshape(1, local_rows), w_query_in, w_query_out, w_item_in, w_item_out)

    return jax.shard_map(local_step, mesh=mesh,
                         in_specs=(P("dp", None), P("dp", None), P("dp"), P(), P(), P(), P()),
                         out_specs=(P(), P(), P(), P(), P()), check_vma=False)
```

time: 992 us -> 99.6 us (0.10)
  waiting for transfers between devices: 773 us -> 0 us
  blocking collectives: 109 us -> 0 us
  Pallas kernels: 0 us -> 92.7 us
  matrix products: 53.3 us -> 0 us
  other arithmetic: 30.8 us -> 0 us
  between operations: 15.6 us -> 2.42 us
    reduce_scatter x1 -> x0, waiting for transfers between devices: 650 us -> none  [local_step(): lax.psum_scatter(d_item_part, 'dp', scatter_dimension=0, tiled=True)]
    pallas_call x0 -> x1, Pallas kernels: none -> 92.7 us  [local_step(): pl.pallas_call(functools.partial(kernel, local_rows * group), out_shape=(...]
    psum x1 -> x0, waiting for transfers between devices: 83.1 us -> none  [local_step(): lax.psum(grad_query_in, 'dp')]
    psum x1 -> x0, blocking collectives: 69.7 us -> none  [local_step(): loss = jnp.reshape(lax.psum(loss_sum, 'dp') / total_rows, (1,))]
    dot_general x11 -> x0, matrix products: 53.3 us -> none  [the longest x1 16.6 us: block_step(): jnp.einsum('qe,ke->qk', query_blk, items_all, preferred_element_type=jnp....]
    all_gather x1 -> x0, waiting for transfers between devices: 40 us -> none  [local_step(): lax.all_gather(v_unit.astype(jnp.bfloat16), 'dp', axis=0, tiled=True)]
    all_gather x1 -> x0, blocking collectives: 38.9 us -> none  [local_step(): logq_all = lax.all_gather(log_q, 'dp', axis=0, tiled=True)]
    reduce_sum x3 -> x0, other arithmetic: 18.8 us -> none  [the longest x1 17.3 us: block_step(): pos_logit = jnp.sum(jnp.where(is_pos, logits, 0.0), axis=1, keepdims=True)]
  transfers between devices with their start and end apart: 3 -> 0, of which waited for: 3 -> 0; matrix products, arithmetic and copies ran while one was open for 2% -> 0% of each run, Pallas kernels for 0% -> 0%
where the time goes in v1:
time: 99.6 us; the launch traced here: 99.4 us
  Pallas kernels  92.7 us (93%)
  local copies, waits for them, and re-layouts  4.27 us (4%)
  between operations  2.42 us (2%)
    pallas_call x1, Pallas kernels, local_step(): pl.pallas_call(functools.partial(kernel, local_rows * group), out_shape=(...  92.7 us
    unnamed x10, local copies, waits for them, and re-layouts  4.27 us

profile of v1, /device:TPU:1, one launch (start us, length us, event | category | flops | bytes accessed | tf_op | source)
XLA Modules:
  0.0 99.4 jit_solution(5910067112508532002)
XLA Ops:
  0.6 92.7 %shard_map.110 = (f32[1]{0:T(128)}, f32[512,256]{1,0:T(8,128)}, f32[256,128]{1,0:T(8,128)}, f32[512,256]{1,0:T(8,128)}, f32[256,128]{1,0:T(8,128)}) custom-call(bf16[256,512]{1,0:T(8,128)(2,1)} %qx.1, bf16[256,512]{1,0:T(8,128)(2,1)} %vx.1, f32[1,256]{1,0:T(1,128)} %bitcast.1, bf16[512,256]{1,0:T(8,128)(2,1)} %wqi.1, bf16[256,128]{1,0:T(8,128)(2,1)} %wqo.1, ...), custom_call_target="tpu_custom_call" | custom-call | tf_op jit(solution)/shard_map/pallas_call | solution.py:345
  94.0 0.0 copy-start.2
  94.0 0.0 copy-start
  94.0 1.9 %copy.18 = f32[512,256]{1,0:T(8,128)} copy(f32[512,256]{1,0:T(8,128)} %get-tuple-element.11) | data formatting | bytes 1048576
  95.9 0.0 copy-done.2
  95.9 0.7 copy.19
  96.6 0.0 copy-done
  96.6 0.0 copy-start.1
  96.6 0.8 copy.20
  97.4 0.2 copy-done.1
  97.6 0.7 copy.21
Async XLA Ops:
  94.0 2.0 %copy-start.2 = (f32[256,128]{1,0:T(8,128)S(1)}, f32[256,128]{1,0:T(8,128)}, u32[]{:S(2)}) copy-start(f32[256,128]{1,0:T(8,128)} %get-tuple-element.12) | copy-start | bytes 393220
  94.0 2.6 %copy-start = (f32[512,256]{1,0:T(8,128)S(1)}, f32[512,256]{1,0:T(8,128)}, u32[]{:S(2)}) copy-start(f32[512,256]{1,0:T(8,128)} %get-tuple-element.13) | copy-start | bytes 1572868
  96.6 1.0 %copy-start.1 = (f32[256,128]{1,0:T(8,128)S(1)}, f32[256,128]{1,0:T(8,128)}, u32[]{:S(2)}) copy-start(f32[256,128]{1,0:T(8,128)} %get-tuple-element.14) | copy-start | bytes 393220

commit v2 on v1

v2 whole, which is shorter than its diff:
```python
import functools

import jax
import jax.numpy as jnp
from jax import lax
from jax.experimental import pallas as pl
from jax.experimental.pallas import tpu as pltpu
from jax.sharding import PartitionSpec as P

TEMP = 0.05
NORM_EPS = 1e-6
LOG2E = 1.4426950408889634
BOUND = 20.25
F32 = jnp.float32
BF16 = jnp.bfloat16
NA, NB, NC = 8, 16, 8
STEP = (0, 1, 3, 2)
BACK = (0, 2, 1, 3)
INV_A = [2 * BACK[s // 2] + s % 2 for s in range(NA)]
INV_B = [4 * BACK[t // 4] + t % 4 for t in range(NB)]


def rel_a(r, s):
    dy = (STEP[r // 2] - STEP[s // 2]) % 4
    return 2 * STEP.index(dy) + (r % 2 + s % 2) % 2


def nt(a, b):
    return lax.dot_general(a, b, (((1,), (1,)), ((), ())), preferred_element_type=F32)


def tn(a, b):
    return lax.dot_general(a, b, (((0,), (0,)), ((), ())), preferred_element_type=F32)


def nn(a, b):
    return jnp.dot(a, b, preferred_element_type=F32)


def forward(x, w_in, w_out, pre_s, hid_s, inv_s, unit_s):
    pre = nn(x[...], w_in[...])
    hid = jnp.maximum(pre, 0.0).astype(BF16)
    emb = nn(hid, w_out[...])
    inv = lax.rsqrt(jnp.sum(emb * emb, axis=-1, keepdims=True) + NORM_EPS)
    unit = emb * inv
    pre_s[...] = pre
    hid_s[...] = hid
    inv_s[...] = jnp.broadcast_to(inv, unit.shape)
    unit_s[...] = unit


def backward(x, w_out, pre_s, hid_s, inv_s, unit_s, d_unit):
    unit = unit_s[...]
    d_emb = inv_s[...] * (d_unit - unit * jnp.sum(unit * d_unit, axis=-1, keepdims=True))
    d_emb = d_emb.astype(BF16)
    g_out = tn(hid_s[...], d_emb)
    d_hid = nt(d_emb, w_out[...])
    d_pre = jnp.where(pre_s[...] > 0, d_hid, 0.0).astype(BF16)
    g_in = tn(x[...], d_pre)
    return g_in, g_out


def kernel(total_rows, qx, vx, lq, wqi, wqo, wvi, wvo,
           loss_o, gqi_o, gqo_o, gvi_o, gvo_o,
           u_all, v_all, lq_all, lows, kcol, e_all, zacc, zs, rz, dut, dur, dvs, dvp, dvc, dvr,
           q_pre, q_hid, q_inv, q_unit, v_pre, v_hid, v_inv, v_unit,
           gq, gv, pq, pv, hq, hv, rq, rv, oq, ov, xq, xv, fq, fv,
           us, ur, vs, vr, ls, lr, lows_s, lows_r, zss, zsr, dus, durs, dvps, dvpr, dvss, dvsr,
           ps, pr, r1s, r1r, r2s, r2r, r3s, r3r, r4s, r4r):
    me = lax.axis_index("dp")
    core = me % 2
    x = (me // 2) % 4
    y = (me // 8) % 4
    z = me // 32
    lo = ((z + 1) // 2) % 2
    hi = z // 2
    scale = 1.0 / (TEMP * total_rows)
    other = (core + 1) % 2
    mate = z * 32 + y * 8 + x * 2 + other

    def a_dev(s):
        zz = z + (s % 2) * (1 - 2 * (z % 2))
        return zz * 32 + ((y + STEP[s // 2]) % 4) * 8 + x * 2 + core

    def c_dev(t, flip=0):
        i = t // 2
        step = STEP[i] if isinstance(t, int) else i + (i // 2) * (1 - 2 * (i % 2))
        zz = z + (t % 2) * (3 - 2 * z)
        return zz * 32 + y * 8 + ((x + step) % 4) * 2 + (core + flip) % 2

    def back_c(t):
        i = t // 2
        return 2 * (i + ((i + 1) // 2) * (3 - 2 * i) * (1 - i // 3)) + t % 2

    def copy(src, dst, ssem, rsem, dev):
        return pltpu.make_async_remote_copy(src_ref=src, dst_ref=dst, send_sem=ssem, recv_sem=rsem,
                                            device_id=(dev,), device_id_type=pl.DeviceIdType.MESH)

    sent = []

    def send(src, dst, ssem, rsem, dev):
        c = copy(src, dst, ssem, rsem, dev)
        c.start()
        sent.append(c)

    def arrived(dst, ssem, rsem):
        copy(dst, dst, ssem, rsem, me).wait_recv()

    barrier = pltpu.get_barrier_semaphore()
    partners = [a_dev(s) for s in range(1, NA)] + [c_dev(t // 2, t % 2) for t in range(1, NB)]
    for dev in partners:
        pl.semaphore_signal(barrier, inc=1, device_id=(dev,), device_id_type=pl.DeviceIdType.MESH)

    forward(vx, wvi, wvo, v_pre, v_hid, v_inv, v_unit)
    v_all[0] = v_unit[...].astype(BF16)
    pl.semaphore_wait(barrier, len(partners))
    for t in range(1, NB):
        send(lq, lq_all.at[INV_B[t]], ls.at[t], lr.at[INV_B[t]], c_dev(t // 2, t % 2))
    forward(qx, wqi, wqo, q_pre, q_hid, q_inv, q_unit)
    ub = q_unit[...].astype(BF16)
    u_all[0, 0] = ub[0:128]
    u_all[1, 0] = ub[128:256]
    send(v_all.at[0], v_all.at[1], vs.at[1], vr.at[1], mate)
    for t in range(1, NC):
        k = INV_A[t]
        send(v_all.at[0], v_all.at[2 * k], vs.at[2 * t], vr.at[2 * k], c_dev(t))
        send(u_all.at[0, 0], u_all.at[0, k], us.at[0, t], ur.at[0, k], a_dev(t))
    for t in range(1, NA):
        k = INV_A[t]
        send(u_all.at[1, 0], u_all.at[1, k], us.at[1, t], ur.at[1, k], a_dev(t))
    lq_all[0] = lq[...]
    zacc[...] = jnp.zeros_like(zacc)

    low = lq[...]
    for t in range(1, NB):
        arrived(lq_all.at[t], ls.at[t], lr.at[t])
        low = jnp.minimum(low, lq_all[t])
    low = jnp.min(low, axis=1, keepdims=True)
    lows[0] = jnp.broadcast_to(low, (1, 128))

    def column(t, c):
        row = LOG2E * ((lq_all[t] - low) + BOUND)
        kcol[t] = jnp.transpose(jnp.broadcast_to(row, (128, 256)))
        return c

    lax.fori_loop(0, NB, column, 0)
    for s in range(1, NA):
        send(lows.at[0], lows.at[INV_A[s]], lows_s.at[s], lows_r.at[INV_A[s]], a_dev(s))
    for s in range(1, NA):
        arrived(u_all.at[0, s], us.at[0, s], ur.at[0, s])

    c2 = LOG2E / TEMP

    def logits(t, h):
        vt = v_all[t]
        kc = kcol[t]
        kc = jnp.concatenate([kc, kc], axis=1)
        for m in range(4):
            um = u_all[h, 2 * m:2 * m + 2].reshape(256, 128)
            e = jnp.exp2(nt(vt, um) * c2 - kc)
            e_all[t, h, m] = e
            zacc[h, m] += jnp.sum(e.reshape(32, 8, 256), axis=0)

    def first(n, c):
        arrived(v_all.at[2 * n], vs.at[2 * n], vr.at[2 * n])
        copy(v_all.at[2 * n], v_all.at[2 * n + 1], vs.at[2 * n + 1], vr.at[2 * n + 1], mate).start()
        logits(2 * n, 0)
        arrived(v_all.at[2 * n - 1], vs.at[2 * n - 1], vr.at[2 * n - 1])
        logits(2 * n - 1, 0)
        return c

    def share(h):
        rows = []
        for m in range(4):
            row = jnp.sum(zacc[h, m], axis=0, keepdims=True)
            rows += [row[:, 0:128], row[:, 128:256]]
        zs[h, 0] = jnp.concatenate(rows, axis=0)

    def share_send(h):
        for s in range(1, NA):
            send(zs.at[h, 0], zs.at[h, INV_A[s]], zss.at[h, s], zsr.at[h, INV_A[s]], a_dev(s))

    logits(0, 0)
    lax.fori_loop(1, NC, first, 0)
    arrived(v_all.at[NB - 1], vs.at[NB - 1], vr.at[NB - 1])
    logits(NB - 1, 0)
    share(0)
    for s in range(1, NA):
        arrived(u_all.at[1, s], us.at[1, s], ur.at[1, s])
    share_send(0)

    def second(n, c):
        logits(2 * n, 1)
        logits(2 * n + 1, 1)
        return c

    lax.fori_loop(0, NC, second, 0)
    share(1)

    ji = lax.broadcasted_iota(jnp.int32, (256, 256), 0)
    qi = lax.broadcasted_iota(jnp.int32, (256, 256), 1)
    own = q_unit[...].astype(BF16).astype(F32) * v_unit[...].astype(BF16).astype(F32)
    pos = jnp.sum(own) / TEMP
    share_send(1)

    def combine(h):
        for s in range(1, NA):
            arrived(zs.at[h, s], zss.at[h, s], zsr.at[h, s])
        tot = []
        for r in range(NA):
            acc = None
            for s in range(NA):
                k = rel_a(r, s)
                term = fac[s] * zs[h, s, k:k + 1, :]
                acc = term if acc is None else acc + term
            tot.append(acc)
        inv = [fac[0] / w for w in tot]
        for m in range(4):
            rz[h, m] = jnp.concatenate([inv[2 * m], inv[2 * m + 1]], axis=1)
        return jnp.log(tot[0])

    def grads(t, h, diag):
        vt = v_all[t]
        dv = None
        for m in range(4):
            p = e_all[t, h, m] * rz[h, m]
            if diag and m == 0:
                p = jnp.where((ji == qi + h * 128) & (qi < 128), p - 1.0, p)
            g = p.astype(BF16)
            d = nn(g, u_all[h, 2 * m:2 * m + 2].reshape(256, 128))
            dv = d if dv is None else dv + d
            du = tn(vt, g)
            if diag:
                dut[h, 2 * m] = du[:, 0:128]
                dut[h, 2 * m + 1] = du[:, 128:256]
            else:
                dut[h, 2 * m] += du[:, 0:128]
                dut[h, 2 * m + 1] += du[:, 128:256]
        if h == 0:
            dvs[t] = dv
        else:
            dvs[t] += dv

    for s in range(1, NA):
        arrived(lows.at[s], lows_s.at[s], lows_r.at[s])
    lowv = [lows[s] for s in range(NA)]
    least = functools.reduce(jnp.minimum, lowv)
    fac = [jnp.exp(least - w) for w in lowv]
    log0 = combine(0)
    grads(0, 0, True)
    grads(1, 0, False)

    def third(n, c):
        grads(2 * n, 0, False)
        grads(2 * n + 1, 0, False)
        return c

    lax.fori_loop(1, NC, third, 0)
    log1 = combine(1)
    for s in range(1, NA):
        send(dut.at[0, s], dur.at[0, INV_A[s]], dus.at[0, s], durs.at[0, INV_A[s]], a_dev(s))

    def mate_copy(t):
        return copy(dvs.at[2 * t + 1], dvp.at[t], dvps.at[t], dvpr.at[t], mate)

    def dv_copy(t):
        return copy(dvc.at[t], dvr.at[back_c(t)], dvss.at[t], dvsr.at[back_c(t)], c_dev(t))

    def dv_sum(t):
        arrived(dvp.at[t], dvps.at[t], dvpr.at[t])
        dvc[t] = dvs[2 * t] + dvp[t]

    grads(0, 1, True)

    def fourth(n, c):
        grads(2 * n + 1, 1, False)

        @pl.when(n > 2)
        def _():
            dv_sum(n - 2)

        grads(2 * n, 1, False)
        mate_copy(n).start()

        @pl.when(n > 2)
        def _():
            dv_copy(n - 2).start()
        return c

    lax.fori_loop(1, NC, fourth, 0)
    grads(1, 1, False)
    for s in range(1, NA):
        send(dut.at[1, s], dur.at[1, INV_A[s]], dus.at[1, s], durs.at[1, INV_A[s]], a_dev(s))
    mate_copy(0).start()
    dv_sum(NC - 2)
    dv_sum(NC - 1)
    dv_copy(jnp.int32(NC - 2)).start()
    loss_rows = ((BOUND - least) * 2.0 + log0 + log1) + (lq[:, 0:128] + lq[:, 128:256])
    loss_loc = jnp.sum(loss_rows, axis=1, keepdims=True) - pos
    dv_copy(jnp.int32(NC - 1)).start()
    dv_sum(0)

    parts = []
    for h in range(2):
        du = dut[h, 0]
        for s in range(1, NA):
            arrived(dur.at[h, s], dus.at[h, s], durs.at[h, s])
            du = du + dur[h, s]
        parts.append(jnp.transpose(du))
    d_unit = jnp.concatenate(parts, axis=0) * scale
    g_in, g_out = backward(qx, wqo, q_pre, q_hid, q_inv, q_unit, d_unit)

    def pack(buf, g_in, g_out):
        buf[0, 0:512, :] = g_in[:, 0:128]
        buf[0, 512:640, :] = g_in[0:128, 128:256]
        buf[1, 0:384, :] = g_in[128:512, 128:256]
        buf[1, 384:640, :] = g_out

    pack(gq, g_in, g_out)
    lt = jnp.broadcast_to(loss_loc, (8, 128))
    gq[0, 640:648, :] = lt
    gq[1, 640:648, :] = lt
    send(gq.at[other], pq, ps.at[0], pr.at[0], mate)

    def add_dv(t, acc):
        arrived(dvr.at[t], dvss.at[t], dvsr.at[t])
        return acc + dvr[t]

    dv = lax.fori_loop(1, NC, add_dv, dvc[0])
    g_in, g_out = backward(vx, wvo, v_pre, v_hid, v_inv, v_unit, dv * scale)
    pack(gv, g_in, g_out)
    send(gv.at[other], pv, ps.at[1], pr.at[1], mate)

    a_me, b_me = y * 2 + lo, x * 2 + hi

    def a_idx(s):
        return ((y + STEP[s // 2]) % 4) * 2 + (lo + s % 2) % 2

    def c_idx(t):
        return ((x + STEP[t // 2]) % 4) * 2 + (hi + t % 2) % 2

    paths = (
        (gq, pq, hq, rq, oq, xq, fq, c_dev, c_idx, b_me, a_dev, 88, 0),
        (gv, pv, hv, rv, ov, xv, fv, a_dev, a_idx, a_me, c_dev, 80, 1),
    )
    for g, p, h, r, o, xx, f, dev1, idx1, mine, dev2, n, w in paths:
        arrived(p, ps.at[w], pr.at[w])
        h[:, 0:80, :] = (g[core, 0:640, :] + p[0:640, :]).reshape(8, 80, 128)
        if n > 80:
            extra = g[core, 640:648, :] + p[640:648, :]
            for k in range(8):
                h[k, 80:88, :] = extra
        for s in range(1, 8):
            k = INV_A[s]
            send(h.at[idx1(s)], r.at[k], r1s.at[w, s], r1r.at[w, k], dev1(s))
    for g, p, h, r, o, xx, f, dev1, idx1, mine, dev2, n, w in paths:
        acc = h[mine]
        for s in range(1, 8):
            arrived(r.at[s], r1s.at[w, s], r1r.at[w, s])
            acc = acc + r[s]
        o[...] = acc
        for s in range(1, 8):
            k = INV_A[s]
            send(o, xx.at[k], r2s.at[w, s], r2r.at[w, k], dev2(s))
    for g, p, h, r, o, xx, f, dev1, idx1, mine, dev2, n, w in paths:
        acc = o[...]
        for s in range(1, 8):
            arrived(xx.at[s], r2s.at[w, s], r2r.at[w, s])
            acc = acc + xx[s]
        f[core, mine] = acc
        for s in range(1, 8):
            k = INV_A[s]
            send(f.at[core, mine], f.at[core, mine], r3s.at[w, s], r3r.at[w, k], dev1(s))
        send(f.at[core, mine], f.at[core, mine], r4s.at[w, 0], r4r.at[w, 0], mate)
        if n > 80:
            loss_o[0] = acc[80, 0] * (1.0 / total_rows)
    for g, p, h, r, o, xx, f, dev1, idx1, mine, dev2, n, w in paths:
        for s in range(1, 8):
            k = idx1(s)
            arrived(f.at[core, k], r3s.at[w, s], r3r.at[w, s])
            send(f.at[core, k], f.at[core, k], r4s.at[w, s], r4r.at[w, s], mate)
    for g, p, h, r, o, xx, f, dev1, idx1, mine, dev2, n, w in paths:
        arrived(f.at[other, mine], r4s.at[w, 0], r4r.at[w, 0])
        for s in range(1, 8):
            arrived(f.at[other, idx1(s)], r4s.at[w, s], r4r.at[w, s])
        go_in, go_out = (gqi_o, gqo_o) if w == 0 else (gvi_o, gvo_o)
        head = f[0, :, 0:80, :].reshape(640, 128)
        tail = f[1, :, 0:80, :].reshape(640, 128)
        go_in[:, 0:128] = head[0:512]
        go_in[0:128, 128:256] = head[512:640]
        go_in[128:512, 128:256] = tail[0:384]
        go_out[...] = tail[384:640]

    for c in sent:
        c.wait_send()

    def drain(t, c):
        copy(v_all.at[2 * t], v_all.at[2 * t + 1], vs.at[2 * t + 1], vr.at[2 * t + 1], mate).wait_send()
        mate_copy(t).wait_send()
        dv_copy(t).wait_send()
        return c

    lax.fori_loop(1, NC, drain, 0)
    mate_copy(0).wait_send()


def emit(*refs):
    sem = refs[-1]
    copies = [pltpu.make_async_copy(refs[i], refs[4 + i], sem.at[i]) for i in range(4)]
    for c in copies:
        c.start()
    for c in copies:
        c.wait()


def solution(mesh):
    group = mesh.shape["dp"]

    def local_step(query_feat, item_feat, log_q, w_query_in, w_query_out, w_item_in, w_item_out):
        local_rows = query_feat.shape[0]
        vm = lambda *s: pltpu.VMEM(s, F32)
        vb = lambda *s: pltpu.VMEM(s, BF16)
        sem = lambda *s: pltpu.SemaphoreType.DMA(s)
        scratch = [
            vb(2, NA, 128, 128), vb(NB, 256, 128), vm(NB, 1, 256), vm(NA, 1, 128), vm(NB, 256, 128),
            vm(NB, 2, 4, 256, 256), vm(2, 4, 8, 256), vm(2, NA, 8, 128), vm(2, 4, 1, 256),
            vm(2, NA, 128, 128), vm(2, NA, 128, 128),
            vm(NB, 256, 128), vm(NC, 256, 128), vm(NC, 256, 128), vm(NC, 256, 128),
            vm(256, 256), vb(256, 256), vm(256, 128), vm(256, 128),
            vm(256, 256), vb(256, 256), vm(256, 128), vm(256, 128),
            vm(2, 648, 128), vm(2, 640, 128), vm(648, 128), vm(640, 128),
            vm(8, 88, 128), vm(8, 80, 128), vm(8, 88, 128), vm(8, 80, 128),
            vm(88, 128), vm(80, 128), vm(8, 88, 128), vm(8, 80, 128),
            vm(2, 8, 88, 128), vm(2, 8, 80, 128),
            sem(2, NA), sem(2, NA), sem(NB), sem(NB), sem(NB), sem(NB), sem(NA), sem(NA), sem(2, NA), sem(2, NA),
            sem(2, NA), sem(2, NA), sem(NC), sem(NC), sem(NC), sem(NC),
            sem(2), sem(2), sem(2, 8), sem(2, 8), sem(2, 8), sem(2, 8), sem(2, 8), sem(2, 8), sem(2, 8), sem(2, 8),
        ]
        vspec = pl.BlockSpec(memory_space=pltpu.VMEM)
        shapes = ((512, 256), (256, 128), (512, 256), (256, 128))
        loss, *grads = pl.pallas_call(
            functools.partial(kernel, local_rows * group),
            out_shape=(jax.ShapeDtypeStruct((1,), F32), *[pltpu.VMEM(s, F32) for s in shapes]),
            in_specs=[vspec] * 7,
            out_specs=(pl.BlockSpec(memory_space=pltpu.SMEM), vspec, vspec, vspec, vspec),
            scratch_shapes=scratch,
            compiler_params=pltpu.CompilerParams(collective_id=0, has_side_effects=True,
                                                 vmem_limit_bytes=56 * 1024 * 1024),
        )(query_feat, item_feat, log_q.reshape(1, local_rows), w_query_in, w_query_out, w_item_in, w_item_out)
        anys = pl.BlockSpec(memory_space=pl.ANY)
        grads = pl.pallas_call(
            emit,
            out_shape=tuple(jax.ShapeDtypeStruct(s, F32) for s in shapes),
            in_specs=[vspec] * 4,
            out_specs=(anys,) * 4,
            scratch_shapes=[sem(4)],
            compiler_params=pltpu.CompilerParams(vmem_limit_bytes=1024 * 1024),
        )(*grads)
        return (loss, *grads)

    return jax.shard_map(local_step, mesh=mesh,
                         in_specs=(P("dp", None), P("dp", None), P("dp"), P(), P(), P(), P()),
                         out_specs=(P(), P(), P(), P(), P()), check_vma=False)
```

time: 99.6 us -> 82.8 us (0.83)
  Pallas kernels: 92.7 us -> 80.3 us
  local copies, waits for them, and re-layouts: 4.27 us -> 0 us
    pallas_call x1, Pallas kernels: 92.7 us -> 79.2 us  [local_step(): pl.pallas_call(functools.partial(kernel, local_rows * group), out_shape=(...]
    unnamed x10 -> x0, local copies, waits for them, and re-layouts: 4.27 us -> none
    pallas_call x0 -> x1, Pallas kernels: none -> 1.08 us  [local_step(): pl.pallas_call(emit, out_shape=tuple((jax.ShapeDtypeStruct(s, F32) for s...]
where the time goes in v2:
time: 82.8 us; the launch traced here: 82.7 us
  Pallas kernels  80.3 us (97%)
  between operations  2.41 us (3%)
    pallas_call x1, Pallas kernels, local_step(): pl.pallas_call(functools.partial(kernel, local_rows * group), out_shape=(...  79.2 us

profile of v2, /device:TPU:1, one launch (start us, length us, event | category | flops | bytes accessed | tf_op | source)
XLA Modules:
  0.0 82.7 jit_solution(7833325704575957029)
XLA Ops:
  0.6 79.2 %shard_map.110 = (f32[1]{0:T(128)}, f32[512,256]{1,0:T(8,128)S(1)}, f32[256,128]{1,0:T(8,128)S(1)}, f32[512,256]{1,0:T(8,128)S(1)}, f32[256,128]{1,0:T(8,128)S(1)}) custom-call(bf16[256,512]{1,0:T(8,128)(2,1)} %qx.1, bf16[256,512]{1,0:T(8,128)(2,1)} %vx.1, f32[1,256]{1,0:T(1,128)} %bitcast.1, bf16[512,256]{1,0:T(8,128)(2,1)} %wqi.1, bf16[256,128]{1,0:T(8,128)(2,1)} %wqo.1, ...), custom_call_target="tpu_custom_call" | custom-call | tf_op jit(solution)/shard_map/pallas_call | solution.py:441
  79.9 1.1 %shard_map.111 = (f32[512,256]{1,0:T(8,128)}, f32[256,128]{1,0:T(8,128)}, f32[512,256]{1,0:T(8,128)}, f32[256,128]{1,0:T(8,128)}) custom-call(f32[512,256]{1,0:T(8,128)S(1)} %get-tuple-element.15.refs_0_, f32[256,128]{1,0:T(8,128)S(1)} %get-tuple-element.16.refs_1_, f32[512,256]{1,0:T(8,128)S(1)} %get-tuple-element.17.refs_2_, ...), custom_call_target="tpu_custom_call" | custom-call | tf_op jit(solution)/shard_map/pallas_call | solution.py:451

commit v3 on v2

v3 whole, which is shorter than its diff:
```python
import functools

import jax
import jax.numpy as jnp
from jax import lax
from jax.experimental import pallas as pl
from jax.experimental.pallas import tpu as pltpu
from jax.sharding import PartitionSpec as P

TEMP = 0.05
NORM_EPS = 1e-6
LOG2E = 1.4426950408889634
BOUND = 20.25
F32 = jnp.float32
BF16 = jnp.bfloat16
NA, NB, NC = 8, 16, 8
STEP = (0, 1, 3, 2)
BACK = (0, 2, 1, 3)
FAR = (7, 6, 3, 5, 2, 4, 1)
INV_A = [2 * BACK[s // 2] + s % 2 for s in range(NA)]
INV_B = [4 * BACK[t // 4] + t % 4 for t in range(NB)]


def rel_a(r, s):
    dy = (STEP[r // 2] - STEP[s // 2]) % 4
    return 2 * STEP.index(dy) + (r % 2 + s % 2) % 2


def nt(a, b):
    return lax.dot_general(a, b, (((1,), (1,)), ((), ())), preferred_element_type=F32)


def tn(a, b):
    return lax.dot_general(a, b, (((0,), (0,)), ((), ())), preferred_element_type=F32)


def nn(a, b):
    return jnp.dot(a, b, preferred_element_type=F32)


def forward(x, w_in, w_out, pre_s, hid_s, inv_s, unit_s):
    pre = nn(x[...], w_in[...])
    hid = jnp.maximum(pre, 0.0).astype(BF16)
    emb = nn(hid, w_out[...])
    inv = lax.rsqrt(jnp.sum(emb * emb, axis=-1, keepdims=True) + NORM_EPS)
    unit = emb * inv
    pre_s[...] = pre
    hid_s[...] = hid
    inv_s[...] = jnp.broadcast_to(inv, unit.shape)
    unit_s[...] = unit


def backward(x, w_out, pre_s, hid_s, inv_s, unit_s, d_unit):
    unit = unit_s[...]
    d_emb = inv_s[...] * (d_unit - unit * jnp.sum(unit * d_unit, axis=-1, keepdims=True))
    d_emb = d_emb.astype(BF16)
    g_out = tn(hid_s[...], d_emb)
    d_hid = nt(d_emb, w_out[...])
    d_pre = jnp.where(pre_s[...] > 0, d_hid, 0.0).astype(BF16)
    g_in = tn(x[...], d_pre)
    return g_in, g_out


def kernel(total_rows, qx_h, vx_h, lq_h, wqi_h, wqo_h, wvi_h, wvo_h,
           loss_o, gqi_o, gqo_o, gvi_o, gvo_o,
           qx, vx, lq, wqi, wqo, wvi, wvo,
           u_all, v_all, lq_all, lows, kcol, e_all, zacc, zs, rz, dut, dur, dvs, dvp, dvc, dvr,
           q_pre, q_hid, q_inv, q_unit, v_pre, v_hid, v_inv, v_unit,
           gq, gv, pq, pv,
           h0, h1, h2, h3, r0, r1, r2, r3, o0, o1, o2, o3, x0, x1, x2, x3, f0, f1, f2, f3,
           ins, us, ur, vs, vr, ls, lr, lows_s, lows_r, zss, zsr, dus, durs, dvps, dvpr, dvss, dvsr,
           ps, pr, rss, rsr):
    me = lax.axis_index("dp")
    core = me % 2
    x = (me // 2) % 4
    y = (me // 8) % 4
    z = me // 32
    lo = ((z + 1) // 2) % 2
    hi = z // 2
    scale = 1.0 / (TEMP * total_rows)
    other = (core + 1) % 2
    mate = z * 32 + y * 8 + x * 2 + other

    def a_dev(s):
        zz = z + (s % 2) * (1 - 2 * (z % 2))
        return zz * 32 + ((y + STEP[s // 2]) % 4) * 8 + x * 2 + core

    def c_dev(t, flip=0):
        i = t // 2
        step = STEP[i] if isinstance(t, int) else i + (i // 2) * (1 - 2 * (i % 2))
        zz = z + (t % 2) * (3 - 2 * z)
        return zz * 32 + y * 8 + ((x + step) % 4) * 2 + (core + flip) % 2

    def back_c(t):
        i = t // 2
        return 2 * (i + ((i + 1) // 2) * (3 - 2 * i) * (1 - i // 3)) + t % 2

    def copy(src, dst, ssem, rsem, dev):
        return pltpu.make_async_remote_copy(src_ref=src, dst_ref=dst, send_sem=ssem, recv_sem=rsem,
                                            device_id=(dev,), device_id_type=pl.DeviceIdType.MESH)

    def send(src, dst, ssem, rsem, dev):
        copy(src, dst, ssem, rsem, dev).start()

    def arrived(dst, rsem):
        copy(dst, dst, rsem, rsem, me).wait_recv()

    def gone(src, ssem):
        copy(src, src, ssem, ssem, me).wait_send()

    barrier = pltpu.get_barrier_semaphore()
    partners = [a_dev(s) for s in range(1, NA)] + [c_dev(t // 2, t % 2) for t in range(1, NB)]
    for dev in partners:
        pl.semaphore_signal(barrier, inc=1, device_id=(dev,), device_id_type=pl.DeviceIdType.MESH)

    loads = [pltpu.make_async_copy(a, b, ins.at[i]) for i, (a, b) in enumerate((
        (vx_h, vx), (wvi_h, wvi), (wvo_h, wvo), (qx_h, qx), (wqi_h, wqi), (wqo_h, wqo), (lq_h, lq)))]
    for c in loads:
        c.start()
    for c in loads[:3]:
        c.wait()
    forward(vx, wvi, wvo, v_pre, v_hid, v_inv, v_unit)
    v_all[0] = v_unit[...].astype(BF16)
    for c in loads[3:]:
        c.wait()
    forward(qx, wqi, wqo, q_pre, q_hid, q_inv, q_unit)
    ub = q_unit[...].astype(BF16)
    u_all[0, 0] = ub[0:128]
    u_all[1, 0] = ub[128:256]
    pl.semaphore_wait(barrier, len(partners))
    for t in (14, 15, 12, 13, 6, 7, 10, 11, 4, 5, 8, 9, 2, 3, 1):
        send(lq, lq_all.at[INV_B[t]], ls, lr, c_dev(t // 2, t % 2))
    send(v_all.at[0], v_all.at[1], vs, vr.at[1], mate)
    for t in FAR:
        k = INV_A[t]
        send(u_all.at[0, 0], u_all.at[0, k], us.at[0], ur.at[0], a_dev(t))
        send(v_all.at[0], v_all.at[2 * k], vs, vr.at[2 * k], c_dev(t))
    for t in FAR:
        k = INV_A[t]
        send(u_all.at[1, 0], u_all.at[1, k], us.at[1], ur.at[1], a_dev(t))
    lq_all[0] = lq[...]
    zacc[...] = jnp.zeros_like(zacc)

    low = lq[...]
    arrived(lq_all.at[1:NB], lr)
    for t in range(1, NB):
        low = jnp.minimum(low, lq_all[t])
    low = jnp.min(low, axis=1, keepdims=True)
    lows[0] = jnp.broadcast_to(low, (1, 128))

    def column(t, c):
        row = LOG2E * ((lq_all[t] - low) + BOUND)
        kcol[t] = jnp.transpose(jnp.broadcast_to(row, (128, 256)))
        return c

    lax.fori_loop(0, NB, column, 0)
    for s in FAR:
        send(lows.at[0], lows.at[INV_A[s]], lows_s, lows_r, a_dev(s))
    arrived(u_all.at[0, 1:NA], ur.at[0])

    c2 = LOG2E / TEMP

    def logits(t, h):
        vt = v_all[t]
        kc = kcol[t]
        kc = jnp.concatenate([kc, kc], axis=1)
        for m in range(4):
            um = u_all[h, 2 * m:2 * m + 2].reshape(256, 128)
            e = jnp.exp2(nt(vt, um) * c2 - kc)
            e_all[t, h, m] = e
            zacc[h, m] += jnp.sum(e.reshape(32, 8, 256), axis=0)

    def first(n, c):
        arrived(v_all.at[2 * n], vr.at[2 * n])
        copy(v_all.at[2 * n], v_all.at[2 * n + 1], vs, vr.at[2 * n + 1], mate).start()
        logits(2 * n, 0)
        arrived(v_all.at[2 * n - 1], vr.at[2 * n - 1])
        logits(2 * n - 1, 0)
        return c

    def share(h):
        rows = []
        for m in range(4):
            row = jnp.sum(zacc[h, m], axis=0, keepdims=True)
            rows += [row[:, 0:128], row[:, 128:256]]
        zs[h, 0] = jnp.concatenate(rows, axis=0)

    def share_send(h):
        for s in FAR:
            send(zs.at[h, 0], zs.at[h, INV_A[s]], zss.at[h], zsr.at[h], a_dev(s))

    logits(0, 0)
    lax.fori_loop(1, NC, first, 0)
    arrived(v_all.at[NB - 1], vr.at[NB - 1])
    logits(NB - 1, 0)
    share(0)
    arrived(u_all.at[1, 1:NA], ur.at[1])
    share_send(0)

    def second(n, c):
        logits(2 * n, 1)
        logits(2 * n + 1, 1)
        return c

    lax.fori_loop(0, NC, second, 0)
    share(1)

    ji = lax.broadcasted_iota(jnp.int32, (256, 256), 0)
    qi = lax.broadcasted_iota(jnp.int32, (256, 256), 1)
    own = q_unit[...].astype(BF16).astype(F32) * v_unit[...].astype(BF16).astype(F32)
    pos = jnp.sum(own) / TEMP
    share_send(1)

    def combine(h):
        arrived(zs.at[h, 1:NA], zsr.at[h])
        tot = []
        for r in range(NA):
            acc = None
            for s in range(NA):
                k = rel_a(r, s)
                term = fac[s] * zs[h, s, k:k + 1, :]
                acc = term if acc is None else acc + term
            tot.append(acc)
        inv = [fac[0] / w for w in tot]
        for m in range(4):
            rz[h, m] = jnp.concatenate([inv[2 * m], inv[2 * m + 1]], axis=1)
        return jnp.log(tot[0])

    def grads(t, h, diag):
        vt = v_all[t]
        dv = None
        for m in range(4):
            p = e_all[t, h, m] * rz[h, m]
            if diag and m == 0:
                p = jnp.where((ji == qi + h * 128) & (qi < 128), p - 1.0, p)
            g = p.astype(BF16)
            d = nn(g, u_all[h, 2 * m:2 * m + 2].reshape(256, 128))
            dv = d if dv is None else dv + d
            du = tn(vt, g)
            if diag:
                dut[h, 2 * m] = du[:, 0:128]
                dut[h, 2 * m + 1] = du[:, 128:256]
            else:
                dut[h, 2 * m] += du[:, 0:128]
                dut[h, 2 * m + 1] += du[:, 128:256]
        if h == 0:
            dvs[t] = dv
        else:
            dvs[t] += dv

    arrived(lows.at[1:NA], lows_r)
    lowv = [lows[s] for s in range(NA)]
    least = functools.reduce(jnp.minimum, lowv)
    fac = [jnp.exp(least - w) for w in lowv]
    log0 = combine(0)
    grads(0, 0, True)
    grads(1, 0, False)

    def third(n, c):
        grads(2 * n, 0, False)
        grads(2 * n + 1, 0, False)
        return c

    lax.fori_loop(1, NC, third, 0)
    log1 = combine(1)
    for s in FAR:
        send(dut.at[0, s], dur.at[0, INV_A[s]], dus.at[0], durs.at[0], a_dev(s))

    def mate_copy(t):
        return copy(dvs.at[2 * t + 1], dvp.at[t], dvps, dvpr.at[t], mate)

    def dv_copy(t):
        return copy(dvc.at[t], dvr.at[back_c(t)], dvss, dvsr, c_dev(t))

    def dv_sum(t):
        arrived(dvp.at[t], dvpr.at[t])
        dvc[t] = dvs[2 * t] + dvp[t]

    grads(0, 1, True)

    def fourth(n, c):
        t = NC - n
        grads(2 * t + 1, 1, False)

        @pl.when(n > 2)
        def _():
            dv_sum(t + 2)

        grads(2 * t, 1, False)
        mate_copy(t).start()

        @pl.when(n > 2)
        def _():
            dv_copy(t + 2).start()
        return c

    lax.fori_loop(1, NC, fourth, 0)
    grads(1, 1, False)
    for s in FAR:
        send(dut.at[1, s], dur.at[1, INV_A[s]], dus.at[1], durs.at[1], a_dev(s))
    mate_copy(0).start()
    dv_sum(2)
    dv_sum(1)
    dv_copy(jnp.int32(2)).start()
    loss_rows = ((BOUND - least) * 2.0 + log0 + log1) + (lq[:, 0:128] + lq[:, 128:256])
    loss_loc = jnp.sum(loss_rows, axis=1, keepdims=True) - pos
    dv_copy(jnp.int32(1)).start()
    dv_sum(0)

    parts = []
    for h in range(2):
        arrived(dur.at[h, 1:NA], durs.at[h])
        du = dut[h, 0]
        for s in range(1, NA):
            du = du + dur[h, s]
        parts.append(jnp.transpose(du))
    d_unit = jnp.concatenate(parts, axis=0) * scale
    g_in, g_out = backward(qx, wqo, q_pre, q_hid, q_inv, q_unit, d_unit)

    def pack(buf, g_in, g_out):
        buf[0, 0:512, :] = g_in[:, 0:128]
        buf[0, 512:640, :] = g_in[0:128, 128:256]
        buf[1, 0:384, :] = g_in[128:512, 128:256]
        buf[1, 384:640, :] = g_out

    pack(gq, g_in, g_out)
    lt = jnp.broadcast_to(loss_loc, (8, 128))
    gq[0, 640:648, :] = lt
    gq[1, 640:648, :] = lt
    send(gq.at[other], pq, ps.at[0], pr.at[0], mate)

    a_me, b_me = y * 2 + lo, x * 2 + hi

    def a_idx(s):
        return ((y + STEP[s // 2]) % 4) * 2 + (lo + s % 2) % 2

    def c_idx(t):
        return ((x + STEP[t // 2]) % 4) * 2 + (hi + t % 2) % 2

    side_a, side_c = (a_dev, a_idx, a_me), (c_dev, c_idx, b_me)
    paths = (
        (0, h0, r0, o0, x0, f0, side_c, side_a),
        (1, h1, r1, o1, x1, f1, side_a, side_c),
        (2, h2, r2, o2, x2, f2, side_a, side_c),
        (3, h3, r3, o3, x3, f3, side_c, side_a),
    )

    def pair(w, g, p):
        arrived(p, pr.at[w])
        for i, h, r, o, xx, f, (dev, idx, mine), _ in paths[2 * w:2 * w + 2]:
            base = 320 * (i % 2)
            h[:, 0:40, :] = (g[core, base:base + 320, :] + p[base:base + 320, :]).reshape(8, 40, 128)
            if i == 0:
                extra = g[core, 640:648, :] + p[640:648, :]
                for n in range(8):
                    h[n, 40:48, :] = extra
        for i, h, r, o, xx, f, (dev, idx, mine), _ in paths[2 * w:2 * w + 2]:
            for s in FAR:
                send(h.at[idx(s)], r.at[INV_A[s]], rss.at[0, i], rsr.at[0, i], dev(s))

    def scatter(w):
        for i, h, r, o, xx, f, (_, _, mine), (dev, _, _) in paths[2 * w:2 * w + 2]:
            arrived(r.at[1:8], rsr.at[0, i])
            acc = h[mine]
            for s in range(1, 8):
                acc = acc + r[s]
            o[...] = acc
            for s in FAR:
                send(o, xx.at[INV_A[s]], rss.at[1, i], rsr.at[1, i], dev(s))

    def exchange(w):
        for i, h, r, o, xx, f, (dev, idx, mine), _ in paths[2 * w:2 * w + 2]:
            arrived(xx.at[1:8], rsr.at[1, i])
            acc = o[...]
            for s in range(1, 8):
                acc = acc + xx[s]
            f[core, mine] = acc
            for s in FAR:
                send(f.at[core, mine], f.at[core, mine], rss.at[2, i], rsr.at[2, i], dev(s))
            if i == 0:
                loss_o[...] = acc[40:48] * (1.0 / total_rows)

    def gather(w):
        for i, h, r, o, xx, f, _, _ in paths[2 * w:2 * w + 2]:
            arrived(r.at[1:8], rsr.at[2, i])
            send(f.at[core], f.at[core], rss.at[3, i], rsr.at[3, i], mate)

    def finish(w, go_in, go_out):
        halves = [[], []]
        for i, h, r, o, xx, f, _, _ in paths[2 * w:2 * w + 2]:
            arrived(h, rsr.at[3, i])
            for c in range(2):
                halves[c].append(f[c, :, 0:40, :].reshape(320, 128))
        head, tail = [jnp.concatenate(c, axis=0) for c in halves]
        go_in[:, 0:128] = head[0:512]
        go_in[0:128, 128:256] = head[512:640]
        go_in[128:512, 128:256] = tail[0:384]
        go_out[...] = tail[384:640]

    pair(0, gq, pq)
    arrived(dvr.at[1:NC], dvsr)
    dv = lax.fori_loop(1, NC, lambda t, acc: acc + dvr[t], dvc[0])
    g_in, g_out = backward(vx, wvo, v_pre, v_hid, v_inv, v_unit, dv * scale)
    pack(gv, g_in, g_out)
    send(gv.at[other], pv, ps.at[1], pr.at[1], mate)
    pair(1, gv, pv)
    scatter(0)
    scatter(1)
    exchange(0)
    exchange(1)
    gather(0)
    finish(0, gqi_o, gqo_o)
    gather(1)
    finish(1, gvi_o, gvo_o)
    gone(lq_all.at[1:NB], ls)
    gone(lows.at[1:NA], lows_s)
    gone(v_all.at[1:NB], vs)
    for h in range(2):
        gone(u_all.at[h, 1:NA], us.at[h])
        gone(zs.at[h, 1:NA], zss.at[h])
        gone(dur.at[h, 1:NA], dus.at[h])
    gone(dvp, dvps)
    gone(dvr.at[1:NC], dvss)
    gone(pq, ps.at[0])
    gone(pv, ps.at[1])
    for i, h, r, o, xx, f, _, _ in paths:
        gone(r.at[1:8], rss.at[0, i])
        gone(xx.at[1:8], rss.at[1, i])
        gone(r.at[1:8], rss.at[2, i])
        gone(h, rss.at[3, i])


def emit(*refs):
    sem = refs[-1]
    copies = [pltpu.make_async_copy(refs[1 + i], refs[6 + i], sem.at[i]) for i in range(4)]
    for c in copies:
        c.start()
    refs[5][0] = refs[0][0, 0]
    for c in copies:
        c.wait()


def solution(mesh):
    group = mesh.shape["dp"]

    def local_step(query_feat, item_feat, log_q, w_query_in, w_query_out, w_item_in, w_item_out):
        local_rows = query_feat.shape[0]
        vm = lambda *s: pltpu.VMEM(s, F32)
        vb = lambda *s: pltpu.VMEM(s, BF16)
        sem = lambda *s: pltpu.SemaphoreType.DMA(s)
        one = pltpu.SemaphoreType.DMA
        scratch = [
            vb(256, 512), vb(256, 512), vm(1, 256), vb(512, 256), vb(256, 128), vb(512, 256), vb(256, 128),
            vb(2, NA, 128, 128), vb(NB, 256, 128), vm(NB, 1, 256), vm(NA, 1, 128), vm(NB, 256, 128),
            vm(NB, 2, 4, 256, 256), vm(2, 4, 8, 256), vm(2, NA, 8, 128), vm(2, 4, 1, 256),
            vm(2, NA, 128, 128), vm(2, NA, 128, 128),
            vm(NB, 256, 128), vm(NC, 256, 128), vm(NC, 256, 128), vm(NC, 256, 128),
            vm(256, 256), vb(256, 256), vm(256, 128), vm(256, 128),
            vm(256, 256), vb(256, 256), vm(256, 128), vm(256, 128),
            vm(2, 648, 128), vm(2, 640, 128), vm(648, 128), vm(640, 128),
            vm(8, 48, 128), vm(8, 40, 128), vm(8, 40, 128), vm(8, 40, 128),
            vm(8, 48, 128), vm(8, 40, 128), vm(8, 40, 128), vm(8, 40, 128),
            vm(48, 128), vm(40, 128), vm(40, 128), vm(40, 128),
            vm(8, 48, 128), vm(8, 40, 128), vm(8, 40, 128), vm(8, 40, 128),
            vm(2, 8, 48, 128), vm(2, 8, 40, 128), vm(2, 8, 40, 128), vm(2, 8, 40, 128),
            sem(7), sem(2), sem(2), one, sem(NB), one, one, one, one, sem(2), sem(2),
            sem(2), sem(2), one, sem(NC), one, one,
            sem(2), sem(2), sem(4, 4), sem(4, 4),
        ]
        vspec = pl.BlockSpec(memory_space=pltpu.VMEM)
        shapes = ((512, 256), (256, 128), (512, 256), (256, 128))
        hbm = pl.BlockSpec(memory_space=pltpu.HBM)
        staged = pl.pallas_call(
            functools.partial(kernel, local_rows * group),
            out_shape=tuple(pltpu.VMEM(s, F32) for s in ((8, 128), *shapes)),
            in_specs=[hbm] * 7,
            out_specs=(vspec,) * 5,
            scratch_shapes=scratch,
            compiler_params=pltpu.CompilerParams(collective_id=0, has_side_effects=True,
                                                 vmem_limit_bytes=56 * 1024 * 1024),
        )(query_feat, item_feat, log_q.reshape(1, local_rows), w_query_in, w_query_out, w_item_in, w_item_out)
        return pl.pallas_call(
            emit,
            out_shape=tuple(jax.ShapeDtypeStruct(s, F32) for s in ((1,), *shapes)),
            in_specs=[vspec] * 5,
            out_specs=(pl.BlockSpec(memory_space=pltpu.SMEM), hbm, hbm, hbm, hbm),
            scratch_shapes=[sem(4)],
            compiler_params=pltpu.CompilerParams(vmem_limit_bytes=1024 * 1024),
        )(*staged)

    return jax.shard_map(local_step, mesh=mesh,
                         in_specs=(P("dp", None), P("dp", None), P("dp"), P(), P(), P(), P()),
                         out_specs=(P(), P(), P(), P(), P()), check_vma=False)
```

time: 82.8 us -> 72 us (0.87)
  Pallas kernels: 80.3 us -> 71.2 us
  between operations: 2.41 us -> 0.64 us
    pallas_call x1, Pallas kernels: 79.2 us -> 69.6 us  [local_step(): pl.pallas_call(functools.partial(kernel, local_rows * group), out_shape=t...]
where the time goes in v3:
time: 72 us; the launch traced here: 71.8 us
  Pallas kernels  71.2 us (99%)
    pallas_call x1, Pallas kernels, local_step(): pl.pallas_call(functools.partial(kernel, local_rows * group), out_shape=t...  69.6 us
    pallas_call x1, Pallas kernels, local_step(): pl.pallas_call(emit, out_shape=tuple((jax.ShapeDtypeStruct(s, F32) for s...  1.6 us

profile of v3, /device:TPU:1, one launch (start us, length us, event | category | flops | bytes accessed | tf_op | source)
XLA Modules:
  0.0 71.8 jit_solution(88442056168812626)
XLA Ops:
  0.6 69.6 %shard_map.110 = (f32[8,128]{1,0:T(8,128)S(1)}, f32[512,256]{1,0:T(8,128)S(1)}, f32[256,128]{1,0:T(8,128)S(1)}, f32[512,256]{1,0:T(8,128)S(1)}, f32[256,128]{1,0:T(8,128)S(1)}) custom-call(bf16[256,512]{1,0:T(8,128)(2,1)} %qx_h.1, bf16[256,512]{1,0:T(8,128)(2,1)} %vx_h.1, f32[1,256]{1,0:T(1,128)} %bitcast.1, bf16[512,256]{1,0:T(8,128)(2,1)} %wqi_h.1, ...), custom_call_target="tpu_custom_call" | custom-call | tf_op jit(solution)/shard_map/pallas_call | solution.py:473
  70.2 1.6 %shard_map.111 = (f32[1]{0:T(128)}, f32[512,256]{1,0:T(8,128)}, f32[256,128]{1,0:T(8,128)}, f32[512,256]{1,0:T(8,128)}, f32[256,128]{1,0:T(8,128)}) custom-call(f32[8,128]{1,0:T(8,128)S(1)} %get-tuple-element.10.refs_0_, f32[512,256]{1,0:T(8,128)S(1)} %get-tuple-element.11.refs_1_, f32[256,128]{1,0:T(8,128)S(1)} %get-tuple-element.12.refs_2_, ...), custom_call_target="tpu_custom_call" | custom-call | tf_op jit(solution)/shard_map/pallas_call | solution.py:482

commit v4 on v3

--- a/solution.py
+++ b/solution.py
@@ -170,14 +170,6 @@
             e_all[t, h, m] = e
             zacc[h, m] += jnp.sum(e.reshape(32, 8, 256), axis=0)
 
-    def first(n, c):
-        arrived(v_all.at[2 * n], vr.at[2 * n])
-        copy(v_all.at[2 * n], v_all.at[2 * n + 1], vs, vr.at[2 * n + 1], mate).start()
-        logits(2 * n, 0)
-        arrived(v_all.at[2 * n - 1], vr.at[2 * n - 1])
-        logits(2 * n - 1, 0)
-        return c
-
     def share(h):
         rows = []
         for m in range(4):
@@ -189,20 +181,42 @@
         for s in FAR:
             send(zs.at[h, 0], zs.at[h, INV_A[s]], zss.at[h], zsr.at[h], a_dev(s))
 
+    arrived(v_all.at[1], vr.at[1])
     logits(0, 0)
-    lax.fori_loop(1, NC, first, 0)
-    arrived(v_all.at[NB - 1], vr.at[NB - 1])
-    logits(NB - 1, 0)
+    logits(1, 0)
+    for t in range(NC - 1, 0, -1):
+        arrived(v_all.at[2 * t], vr.at[2 * t])
+        copy(v_all.at[2 * t], v_all.at[2 * t + 1], vs, vr.at[2 * t + 1], mate).start()
+
+    def first(n, c):
+        logits(14 - 4 * n, 0)
+        logits(12 - 4 * n, 0)
+        return c
+
+    lax.fori_loop(0, 3, first, 0)
+    logits(2, 0)
+
+    def mates(n, c):
+        for i in range(3):
+            t = 15 - 2 * i - 6 * n
+            arrived(v_all.at[t], vr.at[t])
+        for i in range(3):
+            logits(15 - 2 * i - 6 * n, 0)
+        return c
+
+    lax.fori_loop(0, 2, mates, 0)
+    arrived(v_all.at[3], vr.at[3])
+    logits(3, 0)
     share(0)
     arrived(u_all.at[1, 1:NA], ur.at[1])
     share_send(0)
 
     def second(n, c):
-        logits(2 * n, 1)
-        logits(2 * n + 1, 1)
-        return c
-
-    lax.fori_loop(0, NC, second, 0)
+        for i in range(4):
+            logits(4 * n + i, 1)
+        return c
+
+    lax.fori_loop(0, NB // 4, second, 0)
     share(1)
 
     ji = lax.broadcasted_iota(jnp.int32, (256, 256), 0)
@@ -226,7 +240,7 @@
             rz[h, m] = jnp.concatenate([inv[2 * m], inv[2 * m + 1]], axis=1)
         return jnp.log(tot[0])
 
-    def grads(t, h, diag):
+    def grads(t, h, diag, even=False):
         vt = v_all[t]
         dv = None
         for m in range(4):
@@ -245,6 +259,8 @@
                 dut[h, 2 * m + 1] += du[:, 128:256]
         if h == 0:
             dvs[t] = dv
+        elif even:
+            dvc[t // 2] = dvs[t] + dv + dvp[t // 2]
         else:
             dvs[t] += dv
 
@@ -254,14 +270,13 @@
     fac = [jnp.exp(least - w) for w in lowv]
     log0 = combine(0)
     grads(0, 0, True)
-    grads(1, 0, False)
 
     def third(n, c):
-        grads(2 * n, 0, False)
-        grads(2 * n + 1, 0, False)
-        return c
-
-    lax.fori_loop(1, NC, third, 0)
+        for i in range(1, 4):
+            grads(3 * n + i, 0, False)
+        return c
+
+    lax.fori_loop(0, 5, third, 0)
     log1 = combine(1)
     for s in FAR:
         send(dut.at[0, s], dur.at[0, INV_A[s]], dus.at[0], durs.at[0], a_dev(s))
@@ -272,40 +287,51 @@
     def dv_copy(t):
         return copy(dvc.at[t], dvr.at[back_c(t)], dvss, dvsr, c_dev(t))
 
-    def dv_sum(t):
+    grads(0, 1, True)
+
+    def odd(n, c):
+        t = 7 - 2 * n
+
+        @pl.when(n > 0)
+        def _():
+            mate_copy(t + 1).start()
+
+        grads(2 * t + 1, 1, False)
+        grads(2 * t - 1, 1, False)
+        mate_copy(t).start()
+        return c
+
+    lax.fori_loop(0, 4, odd, 0)
+
+    def even(n, c):
+        t = 7 - 2 * n
+
+        @pl.when(n > 0)
+        def _():
+            dv_copy(t + 1).start()
+
+        @pl.when(n == 0)
+        def _():
+            mate_copy(0).start()
+
         arrived(dvp.at[t], dvpr.at[t])
-        dvc[t] = dvs[2 * t] + dvp[t]
-
-    grads(0, 1, True)
-
-    def fourth(n, c):
-        t = NC - n
-        grads(2 * t + 1, 1, False)
-
-        @pl.when(n > 2)
-        def _():
-            dv_sum(t + 2)
-
-        grads(2 * t, 1, False)
-        mate_copy(t).start()
-
-        @pl.when(n > 2)
-        def _():
-            dv_copy(t + 2).start()
-        return c
-
-    lax.fori_loop(1, NC, fourth, 0)
-    grads(1, 1, False)
+        arrived(dvp.at[t - 1], dvpr.at[t - 1])
+        grads(2 * t, 1, False, True)
+        grads(2 * t - 2, 1, False, True)
+        dv_copy(t).start()
+        return c
+
+    lax.fori_loop(0, 3, even, 0)
+    dv_copy(jnp.int32(2)).start()
+    arrived(dvp.at[1], dvpr.at[1])
+    grads(2, 1, False, True)
     for s in FAR:
         send(dut.at[1, s], dur.at[1, INV_A[s]], dus.at[1], durs.at[1], a_dev(s))
-    mate_copy(0).start()
-    dv_sum(2)
-    dv_sum(1)
-    dv_copy(jnp.int32(2)).start()
     loss_rows = ((BOUND - least) * 2.0 + log0 + log1) + (lq[:, 0:128] + lq[:, 128:256])
     loss_loc = jnp.sum(loss_rows, axis=1, keepdims=True) - pos
     dv_copy(jnp.int32(1)).start()
-    dv_sum(0)
+    arrived(dvp.at[0], dvpr.at[0])
+    dvc[0] = dvs[0] + dvp[0]
 
     parts = []
     for h in range(2):
@@ -430,12 +456,13 @@
         gone(h, rss.at[3, i])
 
 
-def emit(*refs):
-    sem = refs[-1]
-    copies = [pltpu.make_async_copy(refs[1 + i], refs[6 + i], sem.at[i]) for i in range(4)]
-    for c in copies:
+def emit(loss, gqi, gqo, gvi, gvo, loss_o, gqi_o, gqo_o, gvi_o, gvo_o, value, sem):
+    pairs = ((value, loss_o), (gqi, gqi_o), (gvi, gvi_o), (gqo, gqo_o), (gvo, gvo_o))
+    copies = [pltpu.make_async_copy(a, b, sem.at[i]) for i, (a, b) in enumerate(pairs)]
+    for c in copies[1:]:
         c.start()
-    refs[5][0] = refs[0][0, 0]
+    value[0] = loss[0, 0]
+    copies[0].start()
     for c in copies:
         c.wait()
 
@@ -483,8 +510,8 @@
             emit,
             out_shape=tuple(jax.ShapeDtypeStruct(s, F32) for s in ((1,), *shapes)),
             in_specs=[vspec] * 5,
-            out_specs=(pl.BlockSpec(memory_space=pltpu.SMEM), hbm, hbm, hbm, hbm),
-            scratch_shapes=[sem(4)],
+            out_specs=(hbm,) * 5,
+            scratch_shapes=[pltpu.SMEM((1,), F32), sem(5)],
             compiler_params=pltpu.CompilerParams(vmem_limit_bytes=1024 * 1024),
         )(*staged)
 

time: 72 us -> 68.2 us (0.947)
  Pallas kernels: 71.2 us -> 67.4 us
    pallas_call x1, Pallas kernels: 69.6 us -> 66.3 us  [local_step(): pl.pallas_call(functools.partial(kernel, local_rows * group), out_shape=t...]
where the time goes in v4:
time: 68.2 us; the launch traced here: 68.1 us
  Pallas kernels  67.4 us (99%)
    pallas_call x1, Pallas kernels, local_step(): pl.pallas_call(functools.partial(kernel, local_rows * group), out_shape=t...  66.3 us

profile of v4, /device:TPU:1, one launch (start us, length us, event | category | flops | bytes accessed | tf_op | source)
XLA Modules:
  0.0 68.1 jit_solution(2373883192910663404)
XLA Ops:
  0.6 66.3 %shard_map.110 = (f32[8,128]{1,0:T(8,128)S(1)}, f32[512,256]{1,0:T(8,128)S(1)}, f32[256,128]{1,0:T(8,128)S(1)}, f32[512,256]{1,0:T(8,128)S(1)}, f32[256,128]{1,0:T(8,128)S(1)}) custom-call(bf16[256,512]{1,0:T(8,128)(2,1)} %qx_h.1, bf16[256,512]{1,0:T(8,128)(2,1)} %vx_h.1, f32[1,256]{1,0:T(1,128)} %bitcast.1, bf16[512,256]{1,0:T(8,128)(2,1)} %wqi_h.1, ...), custom_call_target="tpu_custom_call" | custom-call | tf_op jit(solution)/shard_map/pallas_call | solution.py:500
  67.0 1.1 %shard_map.111 = (f32[1]{0:T(128)}, f32[512,256]{1,0:T(8,128)}, f32[256,128]{1,0:T(8,128)}, f32[512,256]{1,0:T(8,128)}, f32[256,128]{1,0:T(8,128)}) custom-call(f32[8,128]{1,0:T(8,128)S(1)} %get-tuple-element.10.loss, f32[512,256]{1,0:T(8,128)S(1)} %get-tuple-element.11.gqi, f32[256,128]{1,0:T(8,128)S(1)} %get-tuple-element.12.gqo, ...), custom_call_target="tpu_custom_call" | custom-call | tf_op jit(solution)/shard_map/pallas_call | solution.py:509

commit v5 on v4

--- a/solution.py
+++ b/solution.py
@@ -17,8 +17,11 @@
 STEP = (0, 1, 3, 2)
 BACK = (0, 2, 1, 3)
 FAR = (7, 6, 3, 5, 2, 4, 1)
+PEER_C = ((0, 0), (0, 1), (2, 0), (1, 0), (3, 0), (3, 1), (1, 1), (2, 1))
+FAR_C = (7, 6, 5, 2, 4, 3, 1)
+INV_C = (0, 1, 2, 4, 3, 6, 5, 7)
 INV_A = [2 * BACK[s // 2] + s % 2 for s in range(NA)]
-INV_B = [4 * BACK[t // 4] + t % 4 for t in range(NB)]
+INV_B = [2 * INV_C[t // 2] + t % 2 for t in range(NB)]
 
 
 def rel_a(r, s):
@@ -64,11 +67,11 @@
 def kernel(total_rows, qx_h, vx_h, lq_h, wqi_h, wqo_h, wvi_h, wvo_h,
            loss_o, gqi_o, gqo_o, gvi_o, gvo_o,
            qx, vx, lq, wqi, wqo, wvi, wvo,
-           u_all, v_all, lq_all, lows, kcol, e_all, zacc, zs, rz, dut, dur, dvs, dvp, dvc, dvr,
+           u_all, v_all, lq_all, lows, kcol, e_all, zacc, zs, rz, dut, dur, dvs, dvp, dvc, dvr, relay,
            q_pre, q_hid, q_inv, q_unit, v_pre, v_hid, v_inv, v_unit,
            gq, gv, pq, pv,
            h0, h1, h2, h3, r0, r1, r2, r3, o0, o1, o2, o3, x0, x1, x2, x3, f0, f1, f2, f3,
-           ins, us, ur, vs, vr, ls, lr, lows_s, lows_r, zss, zsr, dus, durs, dvps, dvpr, dvss, dvsr,
+           ins, us, ur, vs, vr, ls, lr, lows_s, lows_r, zss, zsr, dus, durs, dvps, dvpr, dvss, dvsr, relay_r,
            ps, pr, rss, rsr):
     me = lax.axis_index("dp")
     core = me % 2
@@ -86,14 +89,8 @@
         return zz * 32 + ((y + STEP[s // 2]) % 4) * 8 + x * 2 + core
 
     def c_dev(t, flip=0):
-        i = t // 2
-        step = STEP[i] if isinstance(t, int) else i + (i // 2) * (1 - 2 * (i % 2))
-        zz = z + (t % 2) * (3 - 2 * z)
-        return zz * 32 + y * 8 + ((x + step) % 4) * 2 + (core + flip) % 2
-
-    def back_c(t):
-        i = t // 2
-        return 2 * (i + ((i + 1) // 2) * (3 - 2 * i) * (1 - i // 3)) + t % 2
+        dx, dh = PEER_C[t]
+        return (z + dh * (3 - 2 * z)) * 32 + y * 8 + ((x + dx) % 4) * 2 + (core + flip) % 2
 
     def copy(src, dst, ssem, rsem, dev):
         return pltpu.make_async_remote_copy(src_ref=src, dst_ref=dst, send_sem=ssem, recv_sem=rsem,
@@ -128,13 +125,13 @@
     u_all[0, 0] = ub[0:128]
     u_all[1, 0] = ub[128:256]
     pl.semaphore_wait(barrier, len(partners))
-    for t in (14, 15, 12, 13, 6, 7, 10, 11, 4, 5, 8, 9, 2, 3, 1):
+    for t in (15, 14, 13, 12, 11, 10, 5, 4, 9, 8, 7, 6, 3, 2, 1):
         send(lq, lq_all.at[INV_B[t]], ls, lr, c_dev(t // 2, t % 2))
     send(v_all.at[0], v_all.at[1], vs, vr.at[1], mate)
-    for t in FAR:
-        k = INV_A[t]
-        send(u_all.at[0, 0], u_all.at[0, k], us.at[0], ur.at[0], a_dev(t))
-        send(v_all.at[0], v_all.at[2 * k], vs, vr.at[2 * k], c_dev(t))
+    for s, t in zip(FAR, FAR_C):
+        k = 2 * INV_C[t]
+        send(u_all.at[0, 0], u_all.at[0, INV_A[s]], us.at[0], ur.at[0], a_dev(s))
+        send(v_all.at[0], v_all.at[k], vs, vr.at[k], c_dev(t))
     for t in FAR:
         k = INV_A[t]
         send(u_all.at[1, 0], u_all.at[1, k], us.at[1], ur.at[1], a_dev(t))
@@ -284,8 +281,11 @@
     def mate_copy(t):
         return copy(dvs.at[2 * t + 1], dvp.at[t], dvps, dvpr.at[t], mate)
 
-    def dv_copy(t):
-        return copy(dvc.at[t], dvr.at[back_c(t)], dvss, dvsr, c_dev(t))
+    def dv_send(t):
+        if t > 5:
+            send(dvc.at[t], relay.at[7 - t], dvss, relay_r.at[7 - t], c_dev(1 if t == 7 else 3))
+        else:
+            send(dvc.at[t], dvr.at[t], dvss, dvsr, c_dev(t))
 
     grads(0, 1, True)
 
@@ -303,38 +303,36 @@
 
     lax.fori_loop(0, 4, odd, 0)
 
-    def even(n, c):
-        t = 7 - 2 * n
-
-        @pl.when(n > 0)
-        def _():
-            dv_copy(t + 1).start()
-
-        @pl.when(n == 0)
-        def _():
-            mate_copy(0).start()
-
+    mate_copy(0).start()
+    for t in (7, 5, 3):
         arrived(dvp.at[t], dvpr.at[t])
         arrived(dvp.at[t - 1], dvpr.at[t - 1])
+        if t < 7:
+            dv_send(t + 1)
         grads(2 * t, 1, False, True)
         grads(2 * t - 2, 1, False, True)
-        dv_copy(t).start()
-        return c
-
-    lax.fori_loop(0, 3, even, 0)
-    dv_copy(jnp.int32(2)).start()
+        dv_send(t)
     arrived(dvp.at[1], dvpr.at[1])
     grads(2, 1, False, True)
     for s in FAR:
         send(dut.at[1, s], dur.at[1, INV_A[s]], dus.at[1], durs.at[1], a_dev(s))
     loss_rows = ((BOUND - least) * 2.0 + log0 + log1) + (lq[:, 0:128] + lq[:, 128:256])
     loss_loc = jnp.sum(loss_rows, axis=1, keepdims=True) - pos
-    dv_copy(jnp.int32(1)).start()
     arrived(dvp.at[0], dvpr.at[0])
     dvc[0] = dvs[0] + dvp[0]
-
-    parts = []
-    for h in range(2):
+    arrived(relay.at[0], relay_r.at[0])
+    dvc[2] += relay[0]
+    arrived(relay.at[1], relay_r.at[1])
+    dv_send(2)
+    dvc[1] += relay[1]
+    du = dut[0, 0]
+    for s in range(1, NA):
+        if s == 1:
+            arrived(dur.at[0, 1:NA], durs.at[0])
+        du = du + dur[0, s]
+    parts = [jnp.transpose(du)]
+    dv_send(1)
+    for h in range(1, 2):
         arrived(dur.at[h, 1:NA], durs.at[h])
         du = dut[h, 0]
         for s in range(1, NA):
@@ -361,9 +359,9 @@
         return ((y + STEP[s // 2]) % 4) * 2 + (lo + s % 2) % 2
 
     def c_idx(t):
-        return ((x + STEP[t // 2]) % 4) * 2 + (hi + t % 2) % 2
-
-    side_a, side_c = (a_dev, a_idx, a_me), (c_dev, c_idx, b_me)
+        return ((x + PEER_C[t][0]) % 4) * 2 + (hi + PEER_C[t][1]) % 2
+
+    side_a, side_c = (a_dev, a_idx, a_me, FAR, INV_A), (c_dev, c_idx, b_me, FAR_C, INV_C)
     paths = (
         (0, h0, r0, o0, x0, f0, side_c, side_a),
         (1, h1, r1, o1, x1, f1, side_a, side_c),
@@ -373,35 +371,35 @@
 
     def pair(w, g, p):
         arrived(p, pr.at[w])
-        for i, h, r, o, xx, f, (dev, idx, mine), _ in paths[2 * w:2 * w + 2]:
+        for i, h, r, o, xx, f, (dev, idx, mine, far, inv), _ in paths[2 * w:2 * w + 2]:
             base = 320 * (i % 2)
             h[:, 0:40, :] = (g[core, base:base + 320, :] + p[base:base + 320, :]).reshape(8, 40, 128)
             if i == 0:
                 extra = g[core, 640:648, :] + p[640:648, :]
                 for n in range(8):
                     h[n, 40:48, :] = extra
-        for i, h, r, o, xx, f, (dev, idx, mine), _ in paths[2 * w:2 * w + 2]:
-            for s in FAR:
-                send(h.at[idx(s)], r.at[INV_A[s]], rss.at[0, i], rsr.at[0, i], dev(s))
+        for i, h, r, o, xx, f, (dev, idx, mine, far, inv), _ in paths[2 * w:2 * w + 2]:
+            for s in far:
+                send(h.at[idx(s)], r.at[inv[s]], rss.at[0, i], rsr.at[0, i], dev(s))
 
     def scatter(w):
-        for i, h, r, o, xx, f, (_, _, mine), (dev, _, _) in paths[2 * w:2 * w + 2]:
+        for i, h, r, o, xx, f, (_, _, mine, _, _), (dev, _, _, far, inv) in paths[2 * w:2 * w + 2]:
             arrived(r.at[1:8], rsr.at[0, i])
             acc = h[mine]
             for s in range(1, 8):
                 acc = acc + r[s]
             o[...] = acc
-            for s in FAR:
-                send(o, xx.at[INV_A[s]], rss.at[1, i], rsr.at[1, i], dev(s))
+            for s in far:
+                send(o, xx.at[inv[s]], rss.at[1, i], rsr.at[1, i], dev(s))
 
     def exchange(w):
-        for i, h, r, o, xx, f, (dev, idx, mine), _ in paths[2 * w:2 * w + 2]:
+        for i, h, r, o, xx, f, (dev, idx, mine, far, inv), _ in paths[2 * w:2 * w + 2]:
             arrived(xx.at[1:8], rsr.at[1, i])
             acc = o[...]
             for s in range(1, 8):
                 acc = acc + xx[s]
             f[core, mine] = acc
-            for s in FAR:
+            for s in far:
                 send(f.at[core, mine], f.at[core, mine], rss.at[2, i], rsr.at[2, i], dev(s))
             if i == 0:
                 loss_o[...] = acc[40:48] * (1.0 / total_rows)
@@ -424,8 +422,8 @@
         go_out[...] = tail[384:640]
 
     pair(0, gq, pq)
-    arrived(dvr.at[1:NC], dvsr)
-    dv = lax.fori_loop(1, NC, lambda t, acc: acc + dvr[t], dvc[0])
+    arrived(dvr.at[1:6], dvsr)
+    dv = lax.fori_loop(1, 6, lambda t, acc: acc + dvr[t], dvc[0])
     g_in, g_out = backward(vx, wvo, v_pre, v_hid, v_inv, v_unit, dv * scale)
     pack(gv, g_in, g_out)
     send(gv.at[other], pv, ps.at[1], pr.at[1], mate)
@@ -481,7 +479,7 @@
             vb(2, NA, 128, 128), vb(NB, 256, 128), vm(NB, 1, 256), vm(NA, 1, 128), vm(NB, 256, 128),
             vm(NB, 2, 4, 256, 256), vm(2, 4, 8, 256), vm(2, NA, 8, 128), vm(2, 4, 1, 256),
             vm(2, NA, 128, 128), vm(2, NA, 128, 128),
-            vm(NB, 256, 128), vm(NC, 256, 128), vm(NC, 256, 128), vm(NC, 256, 128),
+            vm(NB, 256, 128), vm(NC, 256, 128), vm(NC, 256, 128), vm(NC, 256, 128), vm(2, 256, 128),
             vm(256, 256), vb(256, 256), vm(256, 128), vm(256, 128),
             vm(256, 256), vb(256, 256), vm(256, 128), vm(256, 128),
             vm(2, 648, 128), vm(2, 640, 128), vm(648, 128), vm(640, 128),
@@ -491,7 +489,7 @@
             vm(8, 48, 128), vm(8, 40, 128), vm(8, 40, 128), vm(8, 40, 128),
             vm(2, 8, 48, 128), vm(2, 8, 40, 128), vm(2, 8, 40, 128), vm(2, 8, 40, 128),
             sem(7), sem(2), sem(2), one, sem(NB), one, one, one, one, sem(2), sem(2),
-            sem(2), sem(2), one, sem(NC), one, one,
+            sem(2), sem(2), one, sem(NC), one, one, sem(2),
             sem(2), sem(2), sem(4, 4), sem(4, 4),
         ]
         vspec = pl.BlockSpec(memory_space=pltpu.VMEM)

time: 68.2 us -> 66.2 us (0.971)
  Pallas kernels: 67.4 us -> 65.4 us
    pallas_call x1, Pallas kernels: 66.3 us -> 64.3 us  [local_step(): pl.pallas_call(functools.partial(kernel, local_rows * group), out_shape=t...]
where the time goes in v5:
time: 66.2 us; the launch traced here: 66.1 us
  Pallas kernels  65.4 us (99%)
    pallas_call x1, Pallas kernels, local_step(): pl.pallas_call(functools.partial(kernel, local_rows * group), out_shape=t...  64.3 us

profile of v5, /device:TPU:1, one launch (start us, length us, event | category | flops | bytes accessed | tf_op | source)
XLA Modules:
  0.0 66.1 jit_solution(9556703044263990506)
XLA Ops:
  0.6 64.3 %shard_map.110 = (f32[8,128]{1,0:T(8,128)S(1)}, f32[512,256]{1,0:T(8,128)S(1)}, f32[256,128]{1,0:T(8,128)S(1)}, f32[512,256]{1,0:T(8,128)S(1)}, f32[256,128]{1,0:T(8,128)S(1)}) custom-call(bf16[256,512]{1,0:T(8,128)(2,1)} %qx_h.1, bf16[256,512]{1,0:T(8,128)(2,1)} %vx_h.1, f32[1,256]{1,0:T(1,128)} %bitcast.1, bf16[512,256]{1,0:T(8,128)(2,1)} %wqi_h.1, ...), custom_call_target="tpu_custom_call" | custom-call | tf_op jit(solution)/shard_map/pallas_call | solution.py:498
  65.0 1.1 %shard_map.111 = (f32[1]{0:T(128)}, f32[512,256]{1,0:T(8,128)}, f32[256,128]{1,0:T(8,128)}, f32[512,256]{1,0:T(8,128)}, f32[256,128]{1,0:T(8,128)}) custom-call(f32[8,128]{1,0:T(8,128)S(1)} %get-tuple-element.10.loss, f32[512,256]{1,0:T(8,128)S(1)} %get-tuple-element.11.gqi, f32[256,128]{1,0:T(8,128)S(1)} %get-tuple-element.12.gqo, ...), custom_call_target="tpu_custom_call" | custom-call | tf_op jit(solution)/shard_map/pallas_call | solution.py:507

commit v6 on v5

--- a/solution.py
+++ b/solution.py
@@ -17,9 +17,9 @@
 STEP = (0, 1, 3, 2)
 BACK = (0, 2, 1, 3)
 FAR = (7, 6, 3, 5, 2, 4, 1)
-PEER_C = ((0, 0), (0, 1), (2, 0), (1, 0), (3, 0), (3, 1), (1, 1), (2, 1))
-FAR_C = (7, 6, 5, 2, 4, 3, 1)
-INV_C = (0, 1, 2, 4, 3, 6, 5, 7)
+PEER_C = ((0, 0), (0, 1), (2, 0), (3, 1), (1, 0), (3, 0), (1, 1), (2, 1))
+FAR_C = (7, 6, 3, 2, 5, 4, 1)
+INV_C = (0, 1, 2, 6, 5, 4, 3, 7)
 INV_A = [2 * BACK[s // 2] + s % 2 for s in range(NA)]
 INV_B = [2 * INV_C[t // 2] + t % 2 for t in range(NB)]
 
@@ -283,7 +283,7 @@
 
     def dv_send(t):
         if t > 5:
-            send(dvc.at[t], relay.at[7 - t], dvss, relay_r.at[7 - t], c_dev(1 if t == 7 else 3))
+            send(dvc.at[t], relay.at[7 - t], dvss, relay_r.at[7 - t], c_dev(1 if t == 7 else 4))
         else:
             send(dvc.at[t], dvr.at[t], dvss, dvsr, c_dev(t))
 
@@ -318,26 +318,24 @@
         send(dut.at[1, s], dur.at[1, INV_A[s]], dus.at[1], durs.at[1], a_dev(s))
     loss_rows = ((BOUND - least) * 2.0 + log0 + log1) + (lq[:, 0:128] + lq[:, 128:256])
     loss_loc = jnp.sum(loss_rows, axis=1, keepdims=True) - pos
+    arrived(relay.at[0], relay_r.at[0])
+    dvc[2] += relay[0]
     arrived(dvp.at[0], dvpr.at[0])
     dvc[0] = dvs[0] + dvp[0]
-    arrived(relay.at[0], relay_r.at[0])
-    dvc[2] += relay[0]
+    dv_send(2)
     arrived(relay.at[1], relay_r.at[1])
-    dv_send(2)
     dvc[1] += relay[1]
-    du = dut[0, 0]
-    for s in range(1, NA):
-        if s == 1:
-            arrived(dur.at[0, 1:NA], durs.at[0])
-        du = du + dur[0, s]
-    parts = [jnp.transpose(du)]
-    dv_send(1)
-    for h in range(1, 2):
+
+    def sum_du(h):
         arrived(dur.at[h, 1:NA], durs.at[h])
         du = dut[h, 0]
         for s in range(1, NA):
             du = du + dur[h, s]
-        parts.append(jnp.transpose(du))
+        return jnp.transpose(du)
+
+    parts = [sum_du(0)]
+    dv_send(1)
+    parts.append(sum_du(1))
     d_unit = jnp.concatenate(parts, axis=0) * scale
     g_in, g_out = backward(qx, wqo, q_pre, q_hid, q_inv, q_unit, d_unit)
 

time: 66.2 us -> 66 us (level)
  no operation moved by 1% of the time
where the time goes in v6:
time: 66 us; the launch traced here: 65.9 us
  Pallas kernels  65.2 us (99%)
    pallas_call x1, Pallas kernels, local_step(): pl.pallas_call(functools.partial(kernel, local_rows * group), out_shape=t...  64.1 us

profile of v6, /device:TPU:1, one launch (start us, length us, event | category | flops | bytes accessed | tf_op | source)
XLA Modules:
  0.0 65.9 jit_solution(5249391107756705824)
XLA Ops:
  0.6 64.1 %shard_map.110 = (f32[8,128]{1,0:T(8,128)S(1)}, f32[512,256]{1,0:T(8,128)S(1)}, f32[256,128]{1,0:T(8,128)S(1)}, f32[512,256]{1,0:T(8,128)S(1)}, f32[256,128]{1,0:T(8,128)S(1)}) custom-call(bf16[256,512]{1,0:T(8,128)(2,1)} %qx_h.1, bf16[256,512]{1,0:T(8,128)(2,1)} %vx_h.1, f32[1,256]{1,0:T(1,128)} %bitcast.1, bf16[512,256]{1,0:T(8,128)(2,1)} %wqi_h.1, ...), custom_call_target="tpu_custom_call" | custom-call | tf_op jit(solution)/shard_map/pallas_call | solution.py:496
  64.8 1.1 %shard_map.111 = (f32[1]{0:T(128)}, f32[512,256]{1,0:T(8,128)}, f32[256,128]{1,0:T(8,128)}, f32[512,256]{1,0:T(8,128)}, f32[256,128]{1,0:T(8,128)}) custom-call(f32[8,128]{1,0:T(8,128)S(1)} %get-tuple-element.10.loss, f32[512,256]{1,0:T(8,128)S(1)} %get-tuple-element.11.gqi, f32[256,128]{1,0:T(8,128)S(1)} %get-tuple-element.12.gqo, ...), custom_call_target="tpu_custom_call" | custom-call | tf_op jit(solution)/shard_map/pallas_call | solution.py:505

commit v7 on v6

--- a/solution.py
+++ b/solution.py
@@ -145,12 +145,10 @@
     low = jnp.min(low, axis=1, keepdims=True)
     lows[0] = jnp.broadcast_to(low, (1, 128))
 
-    def column(t, c):
-        row = LOG2E * ((lq_all[t] - low) + BOUND)
-        kcol[t] = jnp.transpose(jnp.broadcast_to(row, (128, 256)))
-        return c
-
-    lax.fori_loop(0, NB, column, 0)
+    table = jnp.concatenate([lq_all[t] for t in range(NB)], axis=0)
+    table = jnp.transpose(LOG2E * ((table - low) + BOUND))
+    for t in range(NB):
+        kcol[t] = jnp.broadcast_to(table[:, t:t + 1], (256, 128))
     for s in FAR:
         send(lows.at[0], lows.at[INV_A[s]], lows_s, lows_r, a_dev(s))
     arrived(u_all.at[0, 1:NA], ur.at[0])
@@ -181,29 +179,17 @@
     arrived(v_all.at[1], vr.at[1])
     logits(0, 0)
     logits(1, 0)
-    for t in range(NC - 1, 0, -1):
-        arrived(v_all.at[2 * t], vr.at[2 * t])
-        copy(v_all.at[2 * t], v_all.at[2 * t + 1], vs, vr.at[2 * t + 1], mate).start()
-
-    def first(n, c):
-        logits(14 - 4 * n, 0)
-        logits(12 - 4 * n, 0)
-        return c
-
-    lax.fori_loop(0, 3, first, 0)
-    logits(2, 0)
-
-    def mates(n, c):
-        for i in range(3):
-            t = 15 - 2 * i - 6 * n
-            arrived(v_all.at[t], vr.at[t])
-        for i in range(3):
-            logits(15 - 2 * i - 6 * n, 0)
-        return c
-
-    lax.fori_loop(0, 2, mates, 0)
-    arrived(v_all.at[3], vr.at[3])
-    logits(3, 0)
+    for group in ((6, 1), (4, 7), (3, 2, 5)):
+        for t in group:
+            arrived(v_all.at[2 * t], vr.at[2 * t])
+            copy(v_all.at[2 * t], v_all.at[2 * t + 1], vs, vr.at[2 * t + 1], mate).start()
+        for t in group:
+            logits(2 * t, 0)
+    for group in ((6, 1, 4), (7, 3, 2), (5,)):
+        for t in group:
+            arrived(v_all.at[2 * t + 1], vr.at[2 * t + 1])
+        for t in group:
+            logits(2 * t + 1, 0)
     share(0)
     arrived(u_all.at[1, 1:NA], ur.at[1])
     share_send(0)

time: 66 us -> 65 us (0.985)
  Pallas kernels: 65.2 us -> 64.2 us
    pallas_call x1, Pallas kernels: 64.1 us -> 63.2 us  [local_step(): pl.pallas_call(functools.partial(kernel, local_rows * group), out_shape=t...]
where the time goes in v7:
time: 65 us; the launch traced here: 64.9 us
  Pallas kernels  64.2 us (99%)
    pallas_call x1, Pallas kernels, local_step(): pl.pallas_call(functools.partial(kernel, local_rows * group), out_shape=t...  63.2 us

profile of v7, /device:TPU:1, one launch (start us, length us, event | category | flops | bytes accessed | tf_op | source)
XLA Modules:
  0.0 64.9 jit_solution(10096977533714124247)
XLA Ops:
  0.6 63.2 %shard_map.110 = (f32[8,128]{1,0:T(8,128)S(1)}, f32[512,256]{1,0:T(8,128)S(1)}, f32[256,128]{1,0:T(8,128)S(1)}, f32[512,256]{1,0:T(8,128)S(1)}, f32[256,128]{1,0:T(8,128)S(1)}) custom-call(bf16[256,512]{1,0:T(8,128)(2,1)} %qx_h.1, bf16[256,512]{1,0:T(8,128)(2,1)} %vx_h.1, f32[1,256]{1,0:T(1,128)} %bitcast.1, bf16[512,256]{1,0:T(8,128)(2,1)} %wqi_h.1, ...), custom_call_target="tpu_custom_call" | custom-call | tf_op jit(solution)/shard_map/pallas_call | solution.py:482
  63.8 1.1 %shard_map.111 = (f32[1]{0:T(128)}, f32[512,256]{1,0:T(8,128)}, f32[256,128]{1,0:T(8,128)}, f32[512,256]{1,0:T(8,128)}, f32[256,128]{1,0:T(8,128)}) custom-call(f32[8,128]{1,0:T(8,128)S(1)} %get-tuple-element.10.loss, f32[512,256]{1,0:T(8,128)S(1)} %get-tuple-element.11.gqi, f32[256,128]{1,0:T(8,128)S(1)} %get-tuple-element.12.gqo, ...), custom_call_target="tpu_custom_call" | custom-call | tf_op jit(solution)/shard_map/pallas_call | solution.py:491

commit v8 on v7

--- a/solution.py
+++ b/solution.py
@@ -19,6 +19,8 @@
 FAR = (7, 6, 3, 5, 2, 4, 1)
 PEER_C = ((0, 0), (0, 1), (2, 0), (3, 1), (1, 0), (3, 0), (1, 1), (2, 1))
 FAR_C = (7, 6, 3, 2, 5, 4, 1)
+GROUPS = ((0,), (12, 2), (8, 14), (6, 4, 10), (13, 3, 9), (15, 7, 5), (11,), (1,))
+V_SEM = {s: i for i, g in enumerate(GROUPS) for s in g}
 INV_C = (0, 1, 2, 6, 5, 4, 3, 7)
 INV_A = [2 * BACK[s // 2] + s % 2 for s in range(NA)]
 INV_B = [2 * INV_C[t // 2] + t % 2 for t in range(NB)]
@@ -67,7 +69,7 @@
 def kernel(total_rows, qx_h, vx_h, lq_h, wqi_h, wqo_h, wvi_h, wvo_h,
            loss_o, gqi_o, gqo_o, gvi_o, gvo_o,
            qx, vx, lq, wqi, wqo, wvi, wvo,
-           u_all, v_all, lq_all, lows, kcol, e_all, zacc, zs, rz, dut, dur, dvs, dvp, dvc, dvr, relay,
+           u_all, v_all, lq_all, lows, kcol, e_all, zacc, zs, rz, dut, dur, dvs, dvp, dvc, dvr, relay, v_t,
            q_pre, q_hid, q_inv, q_unit, v_pre, v_hid, v_inv, v_unit,
            gq, gv, pq, pv,
            h0, h1, h2, h3, r0, r1, r2, r3, o0, o1, o2, o3, x0, x1, x2, x3, f0, f1, f2, f3,
@@ -127,11 +129,11 @@
     pl.semaphore_wait(barrier, len(partners))
     for t in (15, 14, 13, 12, 11, 10, 5, 4, 9, 8, 7, 6, 3, 2, 1):
         send(lq, lq_all.at[INV_B[t]], ls, lr, c_dev(t // 2, t % 2))
-    send(v_all.at[0], v_all.at[1], vs, vr.at[1], mate)
+    send(v_all.at[0], v_all.at[1], vs, vr.at[V_SEM[1]], mate)
     for s, t in zip(FAR, FAR_C):
         k = 2 * INV_C[t]
         send(u_all.at[0, 0], u_all.at[0, INV_A[s]], us.at[0], ur.at[0], a_dev(s))
-        send(v_all.at[0], v_all.at[k], vs, vr.at[k], c_dev(t))
+        send(v_all.at[0], v_all.at[k], vs, vr.at[V_SEM[k]], c_dev(t))
     for t in FAR:
         k = INV_A[t]
         send(u_all.at[1, 0], u_all.at[1, k], us.at[1], ur.at[1], a_dev(t))
@@ -176,30 +178,29 @@
         for s in FAR:
             send(zs.at[h, 0], zs.at[h, INV_A[s]], zss.at[h], zsr.at[h], a_dev(s))
 
-    arrived(v_all.at[1], vr.at[1])
+    arrived(v_all.at[1], vr.at[V_SEM[1]])
     logits(0, 0)
     logits(1, 0)
-    for group in ((6, 1), (4, 7), (3, 2, 5)):
+    for i, group in enumerate(GROUPS[1:4]):
+        arrived(v_all.at[0:len(group)], vr.at[i + 1])
         for t in group:
-            arrived(v_all.at[2 * t], vr.at[2 * t])
-            copy(v_all.at[2 * t], v_all.at[2 * t + 1], vs, vr.at[2 * t + 1], mate).start()
+            copy(v_all.at[t], v_all.at[t + 1], vs, vr.at[V_SEM[t + 1]], mate).start()
         for t in group:
-            logits(2 * t, 0)
-    for group in ((6, 1, 4), (7, 3, 2), (5,)):
+            logits(t, 0)
+    for i, group in enumerate(GROUPS[4:7]):
+        arrived(v_all.at[0:len(group)], vr.at[i + 4])
         for t in group:
-            arrived(v_all.at[2 * t + 1], vr.at[2 * t + 1])
-        for t in group:
-            logits(2 * t + 1, 0)
+            logits(t, 0)
     share(0)
     arrived(u_all.at[1, 1:NA], ur.at[1])
     share_send(0)
 
     def second(n, c):
-        for i in range(4):
-            logits(4 * n + i, 1)
+        for i in range(8):
+            logits(8 * n + i, 1)
         return c
 
-    lax.fori_loop(0, NB // 4, second, 0)
+    lax.fori_loop(0, NB // 8, second, 0)
     share(1)
 
     ji = lax.broadcasted_iota(jnp.int32, (256, 256), 0)
@@ -224,7 +225,7 @@
         return jnp.log(tot[0])
 
     def grads(t, h, diag, even=False):
-        vt = v_all[t]
+        vt = v_t[t]
         dv = None
         for m in range(4):
             p = e_all[t, h, m] * rz[h, m]
@@ -233,7 +234,7 @@
             g = p.astype(BF16)
             d = nn(g, u_all[h, 2 * m:2 * m + 2].reshape(256, 128))
             dv = d if dv is None else dv + d
-            du = tn(vt, g)
+            du = nn(vt, g)
             if diag:
                 dut[h, 2 * m] = du[:, 0:128]
                 dut[h, 2 * m + 1] = du[:, 128:256]
@@ -247,6 +248,8 @@
         else:
             dvs[t] += dv
 
+    for t in range(NB):
+        v_t[t] = jnp.transpose(v_all[t])
     arrived(lows.at[1:NA], lows_r)
     lowv = [lows[s] for s in range(NA)]
     least = functools.reduce(jnp.minimum, lowv)
@@ -255,11 +258,11 @@
     grads(0, 0, True)
 
     def third(n, c):
-        for i in range(1, 4):
-            grads(3 * n + i, 0, False)
+        for i in range(1, 6):
+            grads(5 * n + i, 0, False)
         return c
 
-    lax.fori_loop(0, 5, third, 0)
+    lax.fori_loop(0, 3, third, 0)
     log1 = combine(1)
     for s in FAR:
         send(dut.at[0, s], dur.at[0, INV_A[s]], dus.at[0], durs.at[0], a_dev(s))
@@ -463,7 +466,7 @@
             vb(2, NA, 128, 128), vb(NB, 256, 128), vm(NB, 1, 256), vm(NA, 1, 128), vm(NB, 256, 128),
             vm(NB, 2, 4, 256, 256), vm(2, 4, 8, 256), vm(2, NA, 8, 128), vm(2, 4, 1, 256),
             vm(2, NA, 128, 128), vm(2, NA, 128, 128),
-            vm(NB, 256, 128), vm(NC, 256, 128), vm(NC, 256, 128), vm(NC, 256, 128), vm(2, 256, 128),
+            vm(NB, 256, 128), vm(NC, 256, 128), vm(NC, 256, 128), vm(NC, 256, 128), vm(2, 256, 128), vb(NB, 128, 256),
             vm(256, 256), vb(256, 256), vm(256, 128), vm(256, 128),
             vm(256, 256), vb(256, 256), vm(256, 128), vm(256, 128),
             vm(2, 648, 128), vm(2, 640, 128), vm(648, 128), vm(640, 128),
@@ -472,7 +475,7 @@
             vm(48, 128), vm(40, 128), vm(40, 128), vm(40, 128),
             vm(8, 48, 128), vm(8, 40, 128), vm(8, 40, 128), vm(8, 40, 128),
             vm(2, 8, 48, 128), vm(2, 8, 40, 128), vm(2, 8, 40, 128), vm(2, 8, 40, 128),
-            sem(7), sem(2), sem(2), one, sem(NB), one, one, one, one, sem(2), sem(2),
+            sem(7), sem(2), sem(2), one, sem(8), one, one, one, one, sem(2), sem(2),
             sem(2), sem(2), one, sem(NC), one, one, sem(2),
             sem(2), sem(2), sem(4, 4), sem(4, 4),
         ]

time: 65 us -> 64.4 us (level)
  Pallas kernels: 64.2 us -> 63.4 us
    pallas_call x1, Pallas kernels: 63.2 us -> 62.3 us  [local_step(): pl.pallas_call(functools.partial(kernel, local_rows * group), out_shape=t...]
where the time goes in v8:
time: 64.4 us; the launch traced here: 64.2 us
  Pallas kernels  63.4 us (98%)
  between operations  0.8 us (1%)
    pallas_call x1, Pallas kernels, local_step(): pl.pallas_call(functools.partial(kernel, local_rows * group), out_shape=t...  62.3 us

profile of v8, /device:TPU:1, one launch (start us, length us, event | category | flops | bytes accessed | tf_op | source)
XLA Modules:
  0.0 64.2 jit_solution(6432362317470169014)
XLA Ops:
  0.6 62.3 %shard_map.110 = (f32[8,128]{1,0:T(8,128)S(1)}, f32[512,256]{1,0:T(8,128)S(1)}, f32[256,128]{1,0:T(8,128)S(1)}, f32[512,256]{1,0:T(8,128)S(1)}, f32[256,128]{1,0:T(8,128)S(1)}) custom-call(bf16[256,512]{1,0:T(8,128)(2,1)} %qx_h.1, bf16[256,512]{1,0:T(8,128)(2,1)} %vx_h.1, f32[1,256]{1,0:T(1,128)} %bitcast.1, bf16[512,256]{1,0:T(8,128)(2,1)} %wqi_h.1, ...), custom_call_target="tpu_custom_call" | custom-call | tf_op jit(solution)/shard_map/pallas_call | solution.py:485
  63.0 1.1 %shard_map.111 = (f32[1]{0:T(128)}, f32[512,256]{1,0:T(8,128)}, f32[256,128]{1,0:T(8,128)}, f32[512,256]{1,0:T(8,128)}, f32[256,128]{1,0:T(8,128)}) custom-call(f32[8,128]{1,0:T(8,128)S(1)} %get-tuple-element.10.loss, f32[512,256]{1,0:T(8,128)S(1)} %get-tuple-element.11.gqi, f32[256,128]{1,0:T(8,128)S(1)} %get-tuple-element.12.gqo, ...), custom_call_target="tpu_custom_call" | custom-call | tf_op jit(solution)/shard_map/pallas_call | solution.py:494

commit v9 on v8

--- a/solution.py
+++ b/solution.py
@@ -305,7 +305,7 @@
     grads(2, 1, False, True)
     for s in FAR:
         send(dut.at[1, s], dur.at[1, INV_A[s]], dus.at[1], durs.at[1], a_dev(s))
-    loss_rows = ((BOUND - least) * 2.0 + log0 + log1) + (lq[:, 0:128] + lq[:, 128:256])
+    loss_rows = ((lq[:, 0:128] - least) + BOUND + log0) + ((lq[:, 128:256] - least) + BOUND + log1)
     loss_loc = jnp.sum(loss_rows, axis=1, keepdims=True) - pos
     arrived(relay.at[0], relay_r.at[0])
     dvc[2] += relay[0]
@@ -420,8 +420,8 @@
     exchange(0)
     exchange(1)
     gather(0)
+    gather(1)
     finish(0, gqi_o, gqo_o)
-    gather(1)
     finish(1, gvi_o, gvo_o)
     gone(lq_all.at[1:NB], ls)
     gone(lows.at[1:NA], lows_s)

time: 64.4 us -> 64.4 us (level)
  no operation moved by 1% of the time
where the time goes in v9:
time: 64.4 us; the launch traced here: 64.2 us
  Pallas kernels  63.4 us (98%)
  between operations  0.8 us (1%)
    pallas_call x1, Pallas kernels, local_step(): pl.pallas_call(functools.partial(kernel, local_rows * group), out_shape=t...  62.3 us

profile of v9, /device:TPU:1, one launch (start us, length us, event | category | flops | bytes accessed | tf_op | source)
XLA Modules:
  0.0 64.2 jit_solution(1158986770694511030)
XLA Ops:
  0.6 62.3 %shard_map.110 = (f32[8,128]{1,0:T(8,128)S(1)}, f32[512,256]{1,0:T(8,128)S(1)}, f32[256,128]{1,0:T(8,128)S(1)}, f32[512,256]{1,0:T(8,128)S(1)}, f32[256,128]{1,0:T(8,128)S(1)}) custom-call(bf16[256,512]{1,0:T(8,128)(2,1)} %qx_h.1, bf16[256,512]{1,0:T(8,128)(2,1)} %vx_h.1, f32[1,256]{1,0:T(1,128)} %bitcast.1, bf16[512,256]{1,0:T(8,128)(2,1)} %wqi_h.1, ...), custom_call_target="tpu_custom_call" | custom-call | tf_op jit(solution)/shard_map/pallas_call | solution.py:485
  63.0 1.1 %shard_map.111 = (f32[1]{0:T(128)}, f32[512,256]{1,0:T(8,128)}, f32[256,128]{1,0:T(8,128)}, f32[512,256]{1,0:T(8,128)}, f32[256,128]{1,0:T(8,128)}) custom-call(f32[8,128]{1,0:T(8,128)S(1)} %get-tuple-element.10.loss, f32[512,256]{1,0:T(8,128)S(1)} %get-tuple-element.11.gqi, f32[256,128]{1,0:T(8,128)S(1)} %get-tuple-element.12.gqo, ...), custom_call_target="tpu_custom_call" | custom-call | tf_op jit(solution)/shard_map/pallas_call | solution.py:494

commit v10 on v9

--- a/solution.py
+++ b/solution.py
@@ -129,10 +129,11 @@
     pl.semaphore_wait(barrier, len(partners))
     for t in (15, 14, 13, 12, 11, 10, 5, 4, 9, 8, 7, 6, 3, 2, 1):
         send(lq, lq_all.at[INV_B[t]], ls, lr, c_dev(t // 2, t % 2))
+    for s in FAR:
+        send(u_all.at[0, 0], u_all.at[0, INV_A[s]], us.at[0], ur.at[0], a_dev(s))
     send(v_all.at[0], v_all.at[1], vs, vr.at[V_SEM[1]], mate)
-    for s, t in zip(FAR, FAR_C):
+    for t in FAR_C:
         k = 2 * INV_C[t]
-        send(u_all.at[0, 0], u_all.at[0, INV_A[s]], us.at[0], ur.at[0], a_dev(s))
         send(v_all.at[0], v_all.at[k], vs, vr.at[V_SEM[k]], c_dev(t))
     for t in FAR:
         k = INV_A[t]

time: 64.4 us -> 64.4 us (level)
  no operation moved by 1% of the time
where the time goes in v10:
time: 64.4 us; the launch traced here: 64.2 us
  Pallas kernels  63.4 us (98%)
  between operations  0.8 us (1%)
    pallas_call x1, Pallas kernels, local_step(): pl.pallas_call(functools.partial(kernel, local_rows * group), out_shape=t...  62.3 us

profile of v10, /device:TPU:1, one launch (start us, length us, event | category | flops | bytes accessed | tf_op | source)
XLA Modules:
  0.0 64.2 jit_solution(13495800002288891418)
XLA Ops:
  0.6 62.3 %shard_map.110 = (f32[8,128]{1,0:T(8,128)S(1)}, f32[512,256]{1,0:T(8,128)S(1)}, f32[256,128]{1,0:T(8,128)S(1)}, f32[512,256]{1,0:T(8,128)S(1)}, f32[256,128]{1,0:T(8,128)S(1)}) custom-call(bf16[256,512]{1,0:T(8,128)(2,1)} %qx_h.1, bf16[256,512]{1,0:T(8,128)(2,1)} %vx_h.1, f32[1,256]{1,0:T(1,128)} %bitcast.1, bf16[512,256]{1,0:T(8,128)(2,1)} %wqi_h.1, ...), custom_call_target="tpu_custom_call" | custom-call | tf_op jit(solution)/shard_map/pallas_call | solution.py:486
  63.0 1.1 %shard_map.111 = (f32[1]{0:T(128)}, f32[512,256]{1,0:T(8,128)}, f32[256,128]{1,0:T(8,128)}, f32[512,256]{1,0:T(8,128)}, f32[256,128]{1,0:T(8,128)}) custom-call(f32[8,128]{1,0:T(8,128)S(1)} %get-tuple-element.10.loss, f32[512,256]{1,0:T(8,128)S(1)} %get-tuple-element.11.gqi, f32[256,128]{1,0:T(8,128)S(1)} %get-tuple-element.12.gqo, ...), custom_call_target="tpu_custom_call" | custom-call | tf_op jit(solution)/shard_map/pallas_call | solution.py:495

commit v11 on v10

--- a/solution.py
+++ b/solution.py
@@ -269,7 +269,7 @@
         send(dut.at[0, s], dur.at[0, INV_A[s]], dus.at[0], durs.at[0], a_dev(s))
 
     def mate_copy(t):
-        return copy(dvs.at[2 * t + 1], dvp.at[t], dvps, dvpr.at[t], mate)
+        return copy(dvs.at[2 * t + 1], dvp.at[t], dvps, dvpr.at[t // 2], mate)
 
     def dv_send(t):
         if t > 5:
@@ -295,14 +295,13 @@
 
     mate_copy(0).start()
     for t in (7, 5, 3):
-        arrived(dvp.at[t], dvpr.at[t])
-        arrived(dvp.at[t - 1], dvpr.at[t - 1])
+        arrived(dvp.at[t - 1:t + 1], dvpr.at[t // 2])
         if t < 7:
             dv_send(t + 1)
         grads(2 * t, 1, False, True)
         grads(2 * t - 2, 1, False, True)
         dv_send(t)
-    arrived(dvp.at[1], dvpr.at[1])
+    arrived(dvp.at[0:2], dvpr.at[0])
     grads(2, 1, False, True)
     for s in FAR:
         send(dut.at[1, s], dur.at[1, INV_A[s]], dus.at[1], durs.at[1], a_dev(s))
@@ -310,7 +309,6 @@
     loss_loc = jnp.sum(loss_rows, axis=1, keepdims=True) - pos
     arrived(relay.at[0], relay_r.at[0])
     dvc[2] += relay[0]
-    arrived(dvp.at[0], dvpr.at[0])
     dvc[0] = dvs[0] + dvp[0]
     dv_send(2)
     arrived(relay.at[1], relay_r.at[1])
@@ -477,7 +475,7 @@
             vm(8, 48, 128), vm(8, 40, 128), vm(8, 40, 128), vm(8, 40, 128),
             vm(2, 8, 48, 128), vm(2, 8, 40, 128), vm(2, 8, 40, 128), vm(2, 8, 40, 128),
             sem(7), sem(2), sem(2), one, sem(8), one, one, one, one, sem(2), sem(2),
-            sem(2), sem(2), one, sem(NC), one, one, sem(2),
+            sem(2), sem(2), one, sem(4), one, one, sem(2),
             sem(2), sem(2), sem(4, 4), sem(4, 4),
         ]
         vspec = pl.BlockSpec(memory_space=pltpu.VMEM)

time: 64.4 us -> 64.3 us (level)
  no operation moved by 1% of the time
where the time goes in v11:
time: 64.3 us; the launch traced here: 64.2 us
  Pallas kernels  63.4 us (99%)
  between operations  0.8 us (1%)
    pallas_call x1, Pallas kernels, local_step(): pl.pallas_call(functools.partial(kernel, local_rows * group), out_shape=t...  62.3 us

profile of v11, /device:TPU:1, one launch (start us, length us, event | category | flops | bytes accessed | tf_op | source)
XLA Modules:
  0.0 64.2 jit_solution(8309527538787293702)
XLA Ops:
  0.6 62.3 %shard_map.110 = (f32[8,128]{1,0:T(8,128)S(1)}, f32[512,256]{1,0:T(8,128)S(1)}, f32[256,128]{1,0:T(8,128)S(1)}, f32[512,256]{1,0:T(8,128)S(1)}, f32[256,128]{1,0:T(8,128)S(1)}) custom-call(bf16[256,512]{1,0:T(8,128)(2,1)} %qx_h.1, bf16[256,512]{1,0:T(8,128)(2,1)} %vx_h.1, f32[1,256]{1,0:T(1,128)} %bitcast.1, bf16[512,256]{1,0:T(8,128)(2,1)} %wqi_h.1, ...), custom_call_target="tpu_custom_call" | custom-call | tf_op jit(solution)/shard_map/pallas_call | solution.py:484
  62.9 1.1 %shard_map.111 = (f32[1]{0:T(128)}, f32[512,256]{1,0:T(8,128)}, f32[256,128]{1,0:T(8,128)}, f32[512,256]{1,0:T(8,128)}, f32[256,128]{1,0:T(8,128)}) custom-call(f32[8,128]{1,0:T(8,128)S(1)} %get-tuple-element.10.loss, f32[512,256]{1,0:T(8,128)S(1)} %get-tuple-element.11.gqi, f32[256,128]{1,0:T(8,128)S(1)} %get-tuple-element.12.gqo, ...), custom_call_target="tpu_custom_call" | custom-call | tf_op jit(solution)/shard_map/pallas_call | solution.py:493
